TPU v7x, 256 devices: a whole 4x4x8 slice. The times are simulated.
256 devices in a mesh: leaf: 256 (over x, z, y, core).
Axes of the slice: x: 4, y: 4, z: 8, core: 2. Of those that a mesh axis runs over, the one named last changes fastest.
Arguments:
- right_side: float32 [262144, 128], P('leaf'), may hold values from -6 to 6
- diag_blocks: bfloat16 [256, 1024, 1024], P('leaf'), may hold values from -0.1875 to 0.1875
- row_bases: bfloat16 [256, 200, 1024], P('leaf'), may hold values from -0.4375 to 0.4375
- column_bases: bfloat16 [256, 200, 1024], P('leaf'), may hold values from -0.1875 to 0.1875
- transfer: bfloat16 [8, 2, 200, 200], replicated, may hold values from -0.375 to 0.375
- coupling: bfloat16 [8, 2, 200, 200], replicated, may hold values from -0.4375 to 0.4375
- inverse_blocks: bfloat16 [256, 1024, 1024], P('leaf'), may hold values from -0.1875 to 0.1875
- inverse_rows: bfloat16 [256, 200, 1024], P('leaf'), may hold values from -0.4375 to 0.4375
- inverse_columns: bfloat16 [256, 200, 1024], P('leaf'), may hold values from -0.1875 to 0.1875
- inverse_transfer: bfloat16 [8, 2, 200, 200], replicated, may hold values from -0.375 to 0.375
- inverse_coupling: bfloat16 [8, 2, 200, 200], replicated, may hold values from -0.4375 to 0.4375
Outputs:
- solution: float32 [262144, 128], P('leaf')
- hessenberg: float32 [4, 3, 128], replicated
All inputs are finite; a program needn't handle non-finite values.
Results may differ from a plain program's by a relative error of at most 0.0003.
Values sent between devices are 32-bit elements; how exact they have to be, the bound alone decides.
A program may use at most 128 MiB of HBM per device.

v0:
```python
import functools

import jax
import jax.numpy as jnp
from jax import lax
from jax.sharding import Mesh
from jax.sharding import PartitionSpec as P

ITERS = 3
LEAF = ("leaf_0", "leaf_1", "leaf_2", "leaf_3")


EPSILON = 1e-06


def from_partner(block, axis, stride):
    count = lax.axis_size(axis)
    route = []
    for low in range(count):
        high = low | 1 << stride
        if high != low and high < count:
            route += [(low, high), (high, low)]
    return lax.ppermute(block, axis, route)


def over_axes(x, axes):
    return functools.reduce(lax.psum, axes, x)


def transpose_apply(matrix, vectors):
    return lax.dot_general(
        matrix, vectors, (((0,), (0,)), ((), ())), precision=lax.Precision.HIGHEST
    )


def tree_apply(vectors, blocks, row_side, column_side, transfer, coupling, kept_levels):
    levels = transfer.shape[0]
    position = lax.axis_index(LEAF)
    direct = jnp.dot(blocks[0].astype(jnp.float32), vectors, precision=lax.Precision.HIGHEST)
    summary = jnp.dot(column_side[0].astype(jnp.float32), vectors, precision=lax.Precision.HIGHEST)
    lower_depth = levels - min(kept_levels, levels)
    siblings = []
    for height in range(lower_depth):
        partner = from_partner(summary, LEAF, height)
        siblings.append(partner)
        if height < levels - 1:
            parity = position >> height & 1
            left_half = jnp.where(parity == 0, summary, partner)
            right_half = jnp.where(parity == 0, partner, summary)
            translate = transfer[height].astype(jnp.float32)
            summary = transpose_apply(translate[0], left_half) + transpose_apply(
                translate[1], right_half
            )
    downward = None
    for height in reversed(range(levels)):
        parity = position >> height & 1
        bridge = lax.dynamic_index_in_dim(coupling[height], parity, 0, keepdims=False).astype(
            jnp.float32
        )
        incoming = jnp.dot(bridge, siblings[height], precision=lax.Precision.HIGHEST)
        if downward is not None:
            translate = lax.dynamic_index_in_dim(
                transfer[height], parity, 0, keepdims=False
            ).astype(jnp.float32)
            incoming = incoming + jnp.dot(translate, downward, precision=lax.Precision.HIGHEST)
        downward = incoming
    return direct + transpose_apply(row_side[0].astype(jnp.float32), downward)


def least_squares(entries, beta_first):
    unknowns = len(entries[0])
    matrix = [list(line) for line in entries]
    target = [beta_first] + [jnp.zeros_like(beta_first) for column in range(unknowns)]
    for column in range(unknowns):
        upper_entry = matrix[column][column]
        lower_entry = matrix[column + 1][column]
        radius = jnp.sqrt(upper_entry * upper_entry + lower_entry * lower_entry)
        cosine = upper_entry / radius
        sine_value = lower_entry / radius
        for following in range(column, unknowns):
            top_value = matrix[column][following]
            bottom_value = matrix[column + 1][following]
            matrix[column][following] = cosine * top_value + sine_value * bottom_value
            matrix[column + 1][following] = cosine * bottom_value - sine_value * top_value
        top_value = target[column]
        bottom_value = target[column + 1]
        target[column] = cosine * top_value + sine_value * bottom_value
        target[column + 1] = cosine * bottom_value - sine_value * top_value
    coefficients = [None] * unknowns
    for current_row in reversed(range(unknowns)):
        remainder = target[current_row]
        for following in range(current_row + 1, unknowns):
            remainder = remainder - matrix[current_row][following] * coefficients[following]
        coefficients[current_row] = remainder / matrix[current_row][current_row]
    return coefficients


def column_norm(vectors):
    return jnp.sqrt(over_axes(jnp.sum(vectors * vectors, axis=0), LEAF) + EPSILON)


def on_device(
    right_side,
    diag_blocks,
    row_bases,
    column_bases,
    transfer,
    coupling,
    inverse_blocks,
    inverse_rows,
    inverse_columns,
    inverse_transfer,
    inverse_coupling,
):
    kept_levels = 0
    zero_row = jnp.zeros((right_side.shape[1],), jnp.float32)
    entries = [[zero_row for column in range(ITERS)] for line in range(ITERS + 1)]
    images = []
    krylov = []
    candidate = right_side
    beta_first = zero_row
    for column in range(ITERS):
        raw_image = tree_apply(
            candidate,
            inverse_blocks,
            inverse_rows,
            inverse_columns,
            inverse_transfer,
            inverse_coupling,
            kept_levels,
        )
        raw_mixed = tree_apply(
            raw_image, diag_blocks, row_bases, column_bases, transfer, coupling, kept_levels
        )
        partial_value = [jnp.sum(vector * raw_mixed, axis=0) for vector in krylov]
        partial_value = partial_value + [
            jnp.sum(candidate * raw_mixed, axis=0),
            jnp.sum(candidate * candidate, axis=0),
        ]
        totals = over_axes(jnp.stack(partial_value), LEAF)
        norm_value = jnp.sqrt(totals[column + 1] + EPSILON)
        if column == 0:
            beta_first = norm_value
        else:
            entries[column][column - 1] = norm_value
        current = candidate / norm_value
        krylov.append(current)
        images.append(raw_image / norm_value)
        mixed = raw_mixed / norm_value
        correction = jnp.zeros_like(mixed)
        for earlier in range(column):
            product = totals[earlier] / norm_value
            entries[earlier][column] = product
            correction = correction + product * krylov[earlier]
        product = totals[column] / (norm_value * norm_value)
        entries[column][column] = product
        correction = correction + product * current
        candidate = mixed - correction
    entries[ITERS][ITERS - 1] = column_norm(candidate)
    coefficients = least_squares(entries, beta_first)
    solution = jnp.zeros_like(right_side)
    for column in range(ITERS):
        solution = solution + coefficients[column] * images[column]
    hessenberg = jnp.stack([jnp.stack(line) for line in entries])
    return (solution, hessenberg)


def solution(mesh):
    split = Mesh(mesh.devices.reshape(4, 8, 4, 2), ("leaf_0", "leaf_1", "leaf_2", "leaf_3"))
    in_specs = (
        P(LEAF, None),
        P(LEAF, None, None),
        P(LEAF, None, None),
        P(LEAF, None, None),
        P(),
        P(),
        P(LEAF, None, None),
        P(LEAF, None, None),
        P(LEAF, None, None),
        P(),
        P(),
    )
    out_specs = (P(LEAF, None), P())
    return jax.shard_map(
        on_device, mesh=split, in_specs=in_specs, out_specs=out_specs, check_vma=False
    )
```

profile of v0, /device:TPU:1, one launch (start us, length us, event | category | flops | bytes accessed | tf_op | source)
XLA Modules:
  0.0 527.2 jit_solution(4087694463445460252)
XLA Ops:
  9.3 4.1 collective-permute-done.1
  17.2 3.8 collective-permute-done.2
  31.1 4.1 collective-permute-done.4
  37.7 5.3 %collective-permute-start.5 = (f32[200,128]{1,0:T(8,128)S(1)}, f32[200,128]{1,0:T(8,128)S(1)}, u32[]{:S(2)}, u32[]{:S(2)}) collective-permute-start(f32[200,128]{1,0:T(8,128)S(1)} %fusion.74), channel_id=1, source_target_pairs={{0,32},{32,0},{1,33},{33,1},{2,34},{34,2},{3,35},{35,3},{4,36},{36... | collective-permute-start | bytes 307208 | tf_op jit(solution)/shard_map/ppermute | solution.py:23
  74.3 7.2 %collective-permute-start.8 = (f32[200,128]{1,0:T(8,128)S(1)}, f32[200,128]{1,0:T(8,128)S(1)}, u32[]{:S(2)}, u32[]{:S(2)}) collective-permute-start(f32[200,128]{1,0:T(8,128)S(1)} %convolution_bitcast_fusion.5), channel_id=1, source_target_pairs={{0,1},{1,0},{2,3},{3,2},{4,5},{5,4},{6,7},{7,6},{8,9},{9,8},{10,11... | collective-permute-start | bytes 307208 | tf_op jit(solution)/shard_map/ppermute | solution.py:23
  93.9 3.5 collective-permute-done.11
  98.7 4.6 collective-permute-done.12
  103.9 4.9 collective-permute-start.13
  129.9 9.1 %psum.112 = f32[2,128]{1,0:T(2,128)S(1)} all-reduce(f32[2,128]{1,0:T(2,128)S(1)} %pad_maximum_fusion.3), channel_id=1, replica_groups=mesh['leaf_0'=4,'leaf_1'=8,'leaf_2'=4,'leaf_3'=2] {'leaf_0'}, use_global_device_ids=true, to_apply=%region_2.3 | all-reduce | flops 256 | bytes 2048 | tf_op jit(solution)/shard_map/psum | solution.py:27
  138.9 14.4 %psum.113 = f32[2,128]{1,0:T(2,128)S(1)} all-reduce(f32[2,128]{1,0:T(2,128)S(1)} %psum.112), channel_id=1, replica_groups=mesh['leaf_0'=4,'leaf_1'=8,'leaf_2'=4,'leaf_3'=2] {'leaf_1'}, use_global_device_ids=true, to_apply=%region_3.4 | all-reduce | flops 256 | bytes 2048 | tf_op jit(solution)/shard_map/psum | solution.py:27
  153.4 8.7 %psum.114 = f32[2,128]{1,0:T(2,128)S(1)} all-reduce(f32[2,128]{1,0:T(2,128)S(1)} %psum.113), channel_id=1, replica_groups=mesh['leaf_0'=4,'leaf_1'=8,'leaf_2'=4,'leaf_3'=2] {'leaf_2'}, use_global_device_ids=true, to_apply=%region_4.5 | all-reduce | flops 256 | bytes 2048 | tf_op jit(solution)/shard_map/psum | solution.py:27
  162.1 18.5 %psum.115 = f32[2,128]{1,0:T(2,128)S(1)} all-reduce(f32[2,128]{1,0:T(2,128)S(1)} %psum.114), channel_id=1, replica_groups=mesh['leaf_0'=4,'leaf_1'=8,'leaf_2'=4,'leaf_3'=2] {'leaf_3'}, use_global_device_ids=true, to_apply=%region_5.6 | all-reduce | flops 256 | bytes 2048 | tf_op jit(solution)/shard_map/psum | solution.py:27
  186.0 4.1 collective-permute-done.17
  191.4 4.4 collective-permute-done.18
  196.6 3.5 collective-permute-done.19
  200.8 5.2 collective-permute-done.20
  207.5 7.2 %collective-permute-done.21 = f32[200,128]{1,0:T(8,128)S(1)} collective-permute-done((f32[200,128]{1,0:T(8,128)S(1)}, f32[200,128]{1,0:T(8,128)S(1)}, u32[]{:S(2)}, u32[]{:S(2)}) %collective-permute-start.21) | collective-permute-done | bytes 102432 | tf_op jit(solution)/shard_map/ppermute | solution.py:23
  215.5 3.8 collective-permute-done.22
  220.6 4.9 collective-permute-done.23
  232.8 7.4 %collective-permute-start.24 = (f32[200,128]{1,0:T(8,128)S(1)}, f32[200,128]{1,0:T(8,128)S(1)}, u32[]{:S(2)}, u32[]{:S(2)}) collective-permute-start(f32[200,128]{1,0:T(8,128)S(1)} %convolution_bitcast_fusion.3), channel_id=1, source_target_pairs={{0,1},{1,0},{2,3},{3,2},{4,5},{5,4},{6,7},{7,6},{8,9},{9,8},{10,11... | collective-permute-start | bytes 307208 | tf_op jit(solution)/shard_map/ppermute | solution.py:23
  241.9 4.1 collective-permute-done.25
  247.3 4.4 collective-permute-done.26
  252.8 3.5 collective-permute-done.27
  257.1 5.2 collective-permute-done.28
  264.3 7.2 %collective-permute-done.29 = f32[200,128]{1,0:T(8,128)S(1)} collective-permute-done((f32[200,128]{1,0:T(8,128)S(1)}, f32[200,128]{1,0:T(8,128)S(1)}, u32[]{:S(2)}, u32[]{:S(2)}) %collective-permute-start.29) | collective-permute-done | bytes 102432 | tf_op jit(solution)/shard_map/ppermute | solution.py:23
  272.3 3.7 collective-permute-done.30
  277.9 4.6 collective-permute-done.31
  290.7 7.3 %psum.116 = f32[3,128]{1,0:T(4,128)} all-reduce(f32[3,128]{1,0:T(4,128)} %pad_maximum_fusion.1), channel_id=1, replica_groups=mesh['leaf_0'=4,'leaf_1'=8,'leaf_2'=4,'leaf_3'=2] {'leaf_0'}, use_global_device_ids=true, to_apply=%region_9.10 | all-reduce | flops 384 | bytes 3072 | tf_op jit(solution)/shard_map/psum | solution.py:27
  298.0 11.4 %psum.117 = f32[3,128]{1,0:T(4,128)} all-reduce(f32[3,128]{1,0:T(4,128)} %psum.116), channel_id=1, replica_groups=mesh['leaf_0'=4,'leaf_1'=8,'leaf_2'=4,'leaf_3'=2] {'leaf_1'}, use_global_device_ids=true, to_apply=%region_10.11 | all-reduce | flops 384 | bytes 3072 | tf_op jit(solution)/shard_map/psum | solution.py:27
  309.3 7.6 %psum.118 = f32[3,128]{1,0:T(4,128)} all-reduce(f32[3,128]{1,0:T(4,128)} %psum.117), channel_id=1, replica_groups=mesh['leaf_0'=4,'leaf_1'=8,'leaf_2'=4,'leaf_3'=2] {'leaf_2'}, use_global_device_ids=true, to_apply=%region_11.12 | all-reduce | flops 384 | bytes 3072 | tf_op jit(solution)/shard_map/psum | solution.py:27
  316.9 18.0 %psum.119 = f32[3,128]{1,0:T(4,128)} all-reduce(f32[3,128]{1,0:T(4,128)} %psum.118), channel_id=1, replica_groups=mesh['leaf_0'=4,'leaf_1'=8,'leaf_2'=4,'leaf_3'=2] {'leaf_3'}, use_global_device_ids=true, to_apply=%region_12.13 | all-reduce | flops 384 | bytes 3072 | tf_op jit(solution)/shard_map/psum | solution.py:27
  345.6 4.4 collective-permute-done.34
  355.0 5.4 %collective-permute-done.36 = f32[200,128]{1,0:T(8,128)S(1)} collective-permute-done((f32[200,128]{1,0:T(8,128)S(1)}, f32[200,128]{1,0:T(8,128)S(1)}, u32[]{:S(2)}, u32[]{:S(2)}) %collective-permute-start.36) | collective-permute-done | bytes 102432 | tf_op jit(solution)/shard_map/ppermute | solution.py:23
  363.6 5.7 %collective-permute-done.37 = f32[200,128]{1,0:T(8,128)S(1)} collective-permute-done((f32[200,128]{1,0:T(8,128)S(1)}, f32[200,128]{1,0:T(8,128)S(1)}, u32[]{:S(2)}, u32[]{:S(2)}) %collective-permute-start.37) | collective-permute-done | bytes 102432 | tf_op jit(solution)/shard_map/ppermute | solution.py:23
  375.3 5.7 %collective-permute-done.39 = f32[200,128]{0,1:T(8,128)S(1)} collective-permute-done((f32[200,128]{0,1:T(8,128)S(1)}, f32[200,128]{0,1:T(8,128)S(1)}, u32[]{:S(2)}, u32[]{:S(2)}) %collective-permute-start.39) | collective-permute-done | bytes 102432 | tf_op jit(solution)/shard_map/ppermute | solution.py:23
  388.2 6.6 %collective-permute-start.40 = (f32[200,128]{1,0:T(8,128)S(1)}, f32[200,128]{1,0:T(8,128)S(1)}, u32[]{:S(2)}, u32[]{:S(2)}) collective-permute-start(f32[200,128]{1,0:T(8,128)S(1)} %convolution_bitcast_fusion.1), channel_id=1, source_target_pairs={{0,1},{1,0},{2,3},{3,2},{4,5},{5,4},{6,7},{7,6},{8,9},{9,8},{10,11... | collective-permute-start | bytes 307208 | tf_op jit(solution)/shard_map/ppermute | solution.py:23
  402.5 3.9 collective-permute-done.42
  411.4 5.5 %collective-permute-done.44 = f32[200,128]{1,0:T(8,128)S(1)} collective-permute-done((f32[200,128]{1,0:T(8,128)S(1)}, f32[200,128]{1,0:T(8,128)S(1)}, u32[]{:S(2)}, u32[]{:S(2)}) %collective-permute-start.44) | collective-permute-done | bytes 102432 | tf_op jit(solution)/shard_map/ppermute | solution.py:23
  420.4 5.7 %collective-permute-done.45 = f32[200,128]{1,0:T(8,128)S(1)} collective-permute-done((f32[200,128]{1,0:T(8,128)S(1)}, f32[200,128]{1,0:T(8,128)S(1)}, u32[]{:S(2)}, u32[]{:S(2)}) %collective-permute-start.45) | collective-permute-done | bytes 102432 | tf_op jit(solution)/shard_map/ppermute | solution.py:23
  432.8 4.4 collective-permute-done.47
  444.9 8.0 %psum.120 = f32[4,128]{1,0:T(4,128)S(1)} all-reduce(f32[4,128]{1,0:T(4,128)S(1)} %pad_maximum_fusion.2), channel_id=1, replica_groups=mesh['leaf_0'=4,'leaf_1'=8,'leaf_2'=4,'leaf_3'=2] {'leaf_0'}, use_global_device_ids=true, to_apply=%region_17.18 | all-reduce | flops 512 | bytes 4096 | tf_op jit(solution)/shard_map/psum | solution.py:27
  452.8 10.7 %psum.121 = f32[4,128]{1,0:T(4,128)S(1)} all-reduce(f32[4,128]{1,0:T(4,128)S(1)} %psum.120), channel_id=1, replica_groups=mesh['leaf_0'=4,'leaf_1'=8,'leaf_2'=4,'leaf_3'=2] {'leaf_1'}, use_global_device_ids=true, to_apply=%region_18.19 | all-reduce | flops 512 | bytes 4096 | tf_op jit(solution)/shard_map/psum | solution.py:27
  463.5 7.7 %psum.122 = f32[4,128]{1,0:T(4,128)S(1)} all-reduce(f32[4,128]{1,0:T(4,128)S(1)} %psum.121), channel_id=1, replica_groups=mesh['leaf_0'=4,'leaf_1'=8,'leaf_2'=4,'leaf_3'=2] {'leaf_2'}, use_global_device_ids=true, to_apply=%region_19.20 | all-reduce | flops 512 | bytes 4096 | tf_op jit(solution)/shard_map/psum | solution.py:27
  471.1 15.9 %psum.123 = f32[4,128]{1,0:T(4,128)S(1)} all-reduce(f32[4,128]{1,0:T(4,128)S(1)} %psum.122), channel_id=1, replica_groups=mesh['leaf_0'=4,'leaf_1'=8,'leaf_2'=4,'leaf_3'=2] {'leaf_3'}, use_global_device_ids=true, to_apply=%region_20.21 | all-reduce | flops 512 | bytes 4096 | tf_op jit(solution)/shard_map/psum | solution.py:27
  488.6 6.5 %psum.124 = f32[128]{0:T(128)S(1)} all-reduce(f32[128]{0:T(128)S(1)} %multiply_reduce_fusion), channel_id=1, replica_groups=mesh['leaf_0'=4,'leaf_1'=8,'leaf_2'=4,'leaf_3'=2] {'leaf_0'}, use_global_device_ids=true, to_apply=%region_22.23 | all-reduce | flops 128 | bytes 1024 | tf_op jit(solution)/shard_map/psum | solution.py:27
  495.1 12.4 %psum.125 = f32[128]{0:T(128)S(1)} all-reduce(f32[128]{0:T(128)S(1)} %psum.124), channel_id=1, replica_groups=mesh['leaf_0'=4,'leaf_1'=8,'leaf_2'=4,'leaf_3'=2] {'leaf_1'}, use_global_device_ids=true, to_apply=%region_23.24 | all-reduce | flops 128 | bytes 1024 | tf_op jit(solution)/shard_map/psum | solution.py:27
  507.5 6.2 %psum.126 = f32[128]{0:T(128)S(1)} all-reduce(f32[128]{0:T(128)S(1)} %psum.125), channel_id=1, replica_groups=mesh['leaf_0'=4,'leaf_1'=8,'leaf_2'=4,'leaf_3'=2] {'leaf_2'}, use_global_device_ids=true, to_apply=%region_24.25 | all-reduce | flops 128 | bytes 1024 | tf_op jit(solution)/shard_map/psum | solution.py:27
  513.6 10.2 %psum.127 = f32[128]{0:T(128)S(1)} all-reduce(f32[128]{0:T(128)S(1)} %psum.126), channel_id=1, replica_groups=mesh['leaf_0'=4,'leaf_1'=8,'leaf_2'=4,'leaf_3'=2] {'leaf_3'}, use_global_device_ids=true, to_apply=%region_25.26 | all-reduce | flops 128 | bytes 1024 | tf_op jit(solution)/shard_map/psum | solution.py:27
  (542 shorter events, 192.2 us)
Async XLA Ops:
  2.5 4.2 collective-permute-start
  9.2 4.2 collective-permute-start.1
  15.9 5.1 collective-permute-start.2
  23.5 3.6 collective-permute-start.3
  29.5 5.6 %collective-permute-start.4 = (f32[200,128]{1,0:T(8,128)S(1)}, f32[200,128]{1,0:T(8,128)S(1)}, u32[]{:S(2)}, u32[]{:S(2)}) collective-permute-start(f32[200,128]{1,0:T(8,128)S(1)} %fusion.75), channel_id=1, source_target_pairs={{0,16},{16,0},{1,17},{17,1},{2,18},{18,2},{3,19},{19,3},{4,20},{20... | collective-permute-start | bytes 307208 | tf_op jit(solution)/shard_map/ppermute | solution.py:23
  37.7 8.7 %collective-permute-start.5 = (f32[200,128]{1,0:T(8,128)S(1)}, f32[200,128]{1,0:T(8,128)S(1)}, u32[]{:S(2)}, u32[]{:S(2)}) collective-permute-start(f32[200,128]{1,0:T(8,128)S(1)} %fusion.74), channel_id=1, source_target_pairs={{0,32},{32,0},{1,33},{33,1},{2,34},{34,2},{3,35},{35,3},{4,36},{36... | collective-permute-start | bytes 307208 | tf_op jit(solution)/shard_map/ppermute | solution.py:23
  49.5 3.8 collective-permute-start.6
  56.6 5.8 %collective-permute-start.7 = (f32[200,128]{0,1:T(8,128)}, f32[200,128]{0,1:T(8,128)}, u32[]{:S(2)}, u32[]{:S(2)}) collective-permute-start(f32[200,128]{0,1:T(8,128)} %fusion.42), channel_id=1, source_target_pairs={{0,128},{128,0},{1,129},{129,1},{2,130},{130,2},{3,131},{131,3},{4... | collective-permute-start | bytes 307208 | tf_op jit(solution)/shard_map/ppermute | solution.py:23
  74.3 8.2 %collective-permute-start.8 = (f32[200,128]{1,0:T(8,128)S(1)}, f32[200,128]{1,0:T(8,128)S(1)}, u32[]{:S(2)}, u32[]{:S(2)}) collective-permute-start(f32[200,128]{1,0:T(8,128)S(1)} %convolution_bitcast_fusion.5), channel_id=1, source_target_pairs={{0,1},{1,0},{2,3},{3,2},{4,5},{5,4},{6,7},{7,6},{8,9},{9,8},{10,11... | collective-permute-start | bytes 307208 | tf_op jit(solution)/shard_map/ppermute | solution.py:23
  83.2 4.2 collective-permute-start.9
  88.0 5.1 collective-permute-start.10
  93.8 3.6 collective-permute-start.11
  98.0 5.3 %collective-permute-start.12 = (f32[200,128]{1,0:T(8,128)S(1)}, f32[200,128]{1,0:T(8,128)S(1)}, u32[]{:S(2)}, u32[]{:S(2)}) collective-permute-start(f32[200,128]{1,0:T(8,128)S(1)} %fusion.69), channel_id=1, source_target_pairs={{0,16},{16,0},{1,17},{17,1},{2,18},{18,2},{3,19},{19,3},{4,20},{20... | collective-permute-start | bytes 307208 | tf_op jit(solution)/shard_map/ppermute | solution.py:23
  103.9 7.5 %collective-permute-start.13 = (f32[200,128]{1,0:T(8,128)S(1)}, f32[200,128]{1,0:T(8,128)S(1)}, u32[]{:S(2)}, u32[]{:S(2)}) collective-permute-start(f32[200,128]{1,0:T(8,128)S(1)} %fusion.68), channel_id=1, source_target_pairs={{0,32},{32,0},{1,33},{33,1},{2,34},{34,2},{3,35},{35,3},{4,36},{36... | collective-permute-start | bytes 307208 | tf_op jit(solution)/shard_map/ppermute | solution.py:23
  112.1 3.9 collective-permute-start.14
  116.6 5.8 %collective-permute-start.15 = (f32[200,128]{0,1:T(8,128)S(1)}, f32[200,128]{0,1:T(8,128)S(1)}, u32[]{:S(2)}, u32[]{:S(2)}) collective-permute-start(f32[200,128]{0,1:T(8,128)S(1)} %fusion.41), channel_id=1, source_target_pairs={{0,128},{128,0},{1,129},{129,1},{2,130},{130,2},{3,131},{131,3},{4... | collective-permute-start | bytes 307208 | tf_op jit(solution)/shard_map/ppermute | solution.py:23
  183.8 1.4 collective-permute-start.16
  185.9 4.2 collective-permute-start.17
  190.7 5.1 collective-permute-start.18
  196.5 3.6 collective-permute-start.19
  200.7 5.3 %collective-permute-start.20 = (f32[200,128]{1,0:T(8,128)S(1)}, f32[200,128]{1,0:T(8,128)S(1)}, u32[]{:S(2)}, u32[]{:S(2)}) collective-permute-start(f32[200,128]{1,0:T(8,128)S(1)} %fusion.63), channel_id=1, source_target_pairs={{0,16},{16,0},{1,17},{17,1},{2,18},{18,2},{3,19},{19,3},{4,20},{20... | collective-permute-start | bytes 307208 | tf_op jit(solution)/shard_map/ppermute | solution.py:23
  206.7 8.1 %collective-permute-start.21 = (f32[200,128]{1,0:T(8,128)S(1)}, f32[200,128]{1,0:T(8,128)S(1)}, u32[]{:S(2)}, u32[]{:S(2)}) collective-permute-start(f32[200,128]{1,0:T(8,128)S(1)} %fusion.62), channel_id=1, source_target_pairs={{0,32},{32,0},{1,33},{33,1},{2,34},{34,2},{3,35},{35,3},{4,36},{36... | collective-permute-start | bytes 307208 | tf_op jit(solution)/shard_map/ppermute | solution.py:23
  215.4 3.9 collective-permute-start.22
  219.9 5.6 %collective-permute-start.23 = (f32[200,128]{0,1:T(8,128)S(1)}, f32[200,128]{0,1:T(8,128)S(1)}, u32[]{:S(2)}, u32[]{:S(2)}) collective-permute-start(f32[200,128]{0,1:T(8,128)S(1)} %fusion.40), channel_id=1, source_target_pairs={{0,128},{128,0},{1,129},{129,1},{2,130},{130,2},{3,131},{131,3},{4... | collective-permute-start | bytes 307208 | tf_op jit(solution)/shard_map/ppermute | solution.py:23
  232.8 8.3 %collective-permute-start.24 = (f32[200,128]{1,0:T(8,128)S(1)}, f32[200,128]{1,0:T(8,128)S(1)}, u32[]{:S(2)}, u32[]{:S(2)}) collective-permute-start(f32[200,128]{1,0:T(8,128)S(1)} %convolution_bitcast_fusion.3), channel_id=1, source_target_pairs={{0,1},{1,0},{2,3},{3,2},{4,5},{5,4},{6,7},{7,6},{8,9},{9,8},{10,11... | collective-permute-start | bytes 307208 | tf_op jit(solution)/shard_map/ppermute | solution.py:23
  241.8 4.2 collective-permute-start.25
  246.6 5.1 collective-permute-start.26
  252.3 4.0 collective-permute-start.27
  257.0 5.3 %collective-permute-start.28 = (f32[200,128]{1,0:T(8,128)S(1)}, f32[200,128]{1,0:T(8,128)S(1)}, u32[]{:S(2)}, u32[]{:S(2)}) collective-permute-start(f32[200,128]{1,0:T(8,128)S(1)} %fusion.57), channel_id=1, source_target_pairs={{0,16},{16,0},{1,17},{17,1},{2,18},{18,2},{3,19},{19,3},{4,20},{20... | collective-permute-start | bytes 307208 | tf_op jit(solution)/shard_map/ppermute | solution.py:23
  263.0 8.5 %collective-permute-start.29 = (f32[200,128]{1,0:T(8,128)S(1)}, f32[200,128]{1,0:T(8,128)S(1)}, u32[]{:S(2)}, u32[]{:S(2)}) collective-permute-start(f32[200,128]{1,0:T(8,128)S(1)} %fusion.56), channel_id=1, source_target_pairs={{0,32},{32,0},{1,33},{33,1},{2,34},{34,2},{3,35},{35,3},{4,36},{36... | collective-permute-start | bytes 307208 | tf_op jit(solution)/shard_map/ppermute | solution.py:23
  272.2 3.8 collective-permute-start.30
  276.6 6.0 %collective-permute-start.31 = (f32[200,128]{0,1:T(8,128)S(1)}, f32[200,128]{0,1:T(8,128)S(1)}, u32[]{:S(2)}, u32[]{:S(2)}) collective-permute-start(f32[200,128]{0,1:T(8,128)S(1)} %fusion.39), channel_id=1, source_target_pairs={{0,128},{128,0},{1,129},{129,1},{2,130},{130,2},{3,131},{131,3},{4... | collective-permute-start | bytes 307208 | tf_op jit(solution)/shard_map/ppermute | solution.py:23
  338.0 1.4 collective-permute-start.32
  340.1 4.2 collective-permute-start.33
  344.9 5.1 collective-permute-start.34
  350.7 3.6 collective-permute-start.35
  354.9 5.5 %collective-permute-start.36 = (f32[200,128]{1,0:T(8,128)S(1)}, f32[200,128]{1,0:T(8,128)S(1)}, u32[]{:S(2)}, u32[]{:S(2)}) collective-permute-start(f32[200,128]{1,0:T(8,128)S(1)} %fusion.51), channel_id=1, source_target_pairs={{0,16},{16,0},{1,17},{17,1},{2,18},{18,2},{3,19},{19,3},{4,20},{20... | collective-permute-start | bytes 307208 | tf_op jit(solution)/shard_map/ppermute | solution.py:23
  361.1 8.2 %collective-permute-start.37 = (f32[200,128]{1,0:T(8,128)S(1)}, f32[200,128]{1,0:T(8,128)S(1)}, u32[]{:S(2)}, u32[]{:S(2)}) collective-permute-start(f32[200,128]{1,0:T(8,128)S(1)} %fusion.50), channel_id=1, source_target_pairs={{0,32},{32,0},{1,33},{33,1},{2,34},{34,2},{3,35},{35,3},{4,36},{36... | collective-permute-start | bytes 307208 | tf_op jit(solution)/shard_map/ppermute | solution.py:23
  370.0 3.9 collective-permute-start.38
  374.5 6.5 %collective-permute-start.39 = (f32[200,128]{0,1:T(8,128)S(1)}, f32[200,128]{0,1:T(8,128)S(1)}, u32[]{:S(2)}, u32[]{:S(2)}) collective-permute-start(f32[200,128]{0,1:T(8,128)S(1)} %fusion.38), channel_id=1, source_target_pairs={{0,128},{128,0},{1,129},{129,1},{2,130},{130,2},{3,131},{131,3},{4... | collective-permute-start | bytes 307208 | tf_op jit(solution)/shard_map/ppermute | solution.py:23
  388.2 7.6 %collective-permute-start.40 = (f32[200,128]{1,0:T(8,128)S(1)}, f32[200,128]{1,0:T(8,128)S(1)}, u32[]{:S(2)}, u32[]{:S(2)}) collective-permute-start(f32[200,128]{1,0:T(8,128)S(1)} %convolution_bitcast_fusion.1), channel_id=1, source_target_pairs={{0,1},{1,0},{2,3},{3,2},{4,5},{5,4},{6,7},{7,6},{8,9},{9,8},{10,11... | collective-permute-start | bytes 307208 | tf_op jit(solution)/shard_map/ppermute | solution.py:23
  396.5 4.2 collective-permute-start.41
  401.3 5.1 collective-permute-start.42
  407.0 3.6 collective-permute-start.43
  411.3 5.6 %collective-permute-start.44 = (f32[200,128]{1,0:T(8,128)S(1)}, f32[200,128]{1,0:T(8,128)S(1)}, u32[]{:S(2)}, u32[]{:S(2)}) collective-permute-start(f32[200,128]{1,0:T(8,128)S(1)} %fusion.45), channel_id=1, source_target_pairs={{0,16},{16,0},{1,17},{17,1},{2,18},{18,2},{3,19},{19,3},{4,20},{20... | collective-permute-start | bytes 307208 | tf_op jit(solution)/shard_map/ppermute | solution.py:23
  417.6 8.6 %collective-permute-start.45 = (f32[200,128]{1,0:T(8,128)S(1)}, f32[200,128]{1,0:T(8,128)S(1)}, u32[]{:S(2)}, u32[]{:S(2)}) collective-permute-start(f32[200,128]{1,0:T(8,128)S(1)} %fusion.44), channel_id=1, source_target_pairs={{0,32},{32,0},{1,33},{33,1},{2,34},{34,2},{3,35},{35,3},{4,36},{36... | collective-permute-start | bytes 307208 | tf_op jit(solution)/shard_map/ppermute | solution.py:23
  426.8 3.9 collective-permute-start.46
  431.3 5.9 %collective-permute-start.47 = (f32[200,128]{0,1:T(8,128)S(1)}, f32[200,128]{0,1:T(8,128)S(1)}, u32[]{:S(2)}, u32[]{:S(2)}) collective-permute-start(f32[200,128]{0,1:T(8,128)S(1)} %fusion.37), channel_id=1, source_target_pairs={{0,128},{128,0},{1,129},{129,1},{2,130},{130,2},{3,131},{131,3},{4... | collective-permute-start | bytes 307208 | tf_op jit(solution)/shard_map/ppermute | solution.py:23
  (132 other events, 2040.4 us)
where the time goes:
time: 536 us; the launch traced here: 527 us
  blocking collectives  173 us (32%)
  waiting for transfers between devices  167 us (31%)
  matrix products  94.4 us (18%)
  starting transfers between devices  73.4 us (14%)
  other arithmetic  8.21 us (2%)
  local copies, waits for them, and re-layouts  7.06 us (1%)
    psum x16, blocking collectives, over_axes(): return functools.reduce(lax.psum, axes, x)  173 us
    ppermute x48, waiting for transfers between devices, from_partner(): return lax.ppermute(block, axis, route)  167 us
    ppermute x48, starting transfers between devices, from_partner(): return lax.ppermute(block, axis, route)  73.4 us
    dot_general x90, matrix products, transpose_apply(): lax.dot_general(matrix, vectors, (((0,), (0,)), ((), ())), precision=lax....  44.6 us
    dot_general x48, matrix products, tree_apply(): jnp.dot(bridge, siblings[height], precision=lax.Precision.HIGHEST)  16.8 us
    dot_general x6, matrix products, tree_apply(): jnp.dot(blocks[0].astype(jnp.float32), vectors, precision=lax.Precision.H...  15.1 us
    dot_general x42, matrix products, tree_apply(): jnp.dot(translate, downward, precision=lax.Precision.HIGHEST)  12.4 us
  transfers between devices with their start and end apart: 48, of which 46 were waited for; matrix products, arithmetic and copies ran while one was open for 2% of the time, Pallas kernels for 0%

commit v1 on v0

v1 whole, which is shorter than its diff:
```python
import jax
import jax.numpy as jnp
from jax import lax
from jax.experimental import pallas as pl
from jax.experimental.pallas import tpu as pltpu
from jax.sharding import PartitionSpec as P

F32 = jnp.float32
BF16 = jnp.bfloat16
MESH = pl.DeviceIdType.MESH

ITERS = 3
EPSILON = 1e-06
WIDTH = 1024
RANK = 200
LANES = 256
COLS = 128
GROUP = 8
DEEP = 8
OUTER = 4
SLICE = COLS // GROUP
LEVELS = 8
TILE = 256

NT = (((1,), (1,)), ((), ()))
NN = (((1,), (0,)), ((), ()))


def halves(x):
    high = x.astype(BF16)
    return high, (x - high.astype(F32)).astype(BF16)


def product_rows(x, weight, dims):
    rows = x.shape[0]
    high, low = halves(x)
    both = lax.dot_general(
        jnp.concatenate([high, low], axis=0), weight, dims, preferred_element_type=F32
    )
    return both[:rows] + both[rows:]


def pairs(x):
    count = x.shape[0] // 2
    split = x.reshape(count, 2, SLICE, LANES)
    left = split[:, 0].reshape(count * SLICE, LANES)
    right = split[:, 1].reshape(count * SLICE, LANES)
    return left, right


def least_squares(entries, beta_first):
    unknowns = len(entries[0])
    matrix = [list(line) for line in entries]
    target = [beta_first] + [jnp.zeros_like(beta_first) for column in range(unknowns)]
    for column in range(unknowns):
        upper_entry = matrix[column][column]
        lower_entry = matrix[column + 1][column]
        radius = jnp.sqrt(upper_entry * upper_entry + lower_entry * lower_entry)
        cosine = upper_entry / radius
        sine_value = lower_entry / radius
        for following in range(column, unknowns):
            top_value = matrix[column][following]
            bottom_value = matrix[column + 1][following]
            matrix[column][following] = cosine * top_value + sine_value * bottom_value
            matrix[column + 1][following] = cosine * bottom_value - sine_value * top_value
        top_value = target[column]
        bottom_value = target[column + 1]
        target[column] = cosine * top_value + sine_value * bottom_value
        target[column + 1] = cosine * bottom_value - sine_value * top_value
    coefficients = [None] * unknowns
    for current_row in reversed(range(unknowns)):
        remainder = target[current_row]
        for following in range(current_row + 1, unknowns):
            remainder = remainder - matrix[current_row][following] * coefficients[following]
        coefficients[current_row] = remainder / matrix[current_row][current_row]
    return coefficients


def kernel(
    rhs_hbm,
    ea_hbm,
    pa_hbm,
    qa_hbm,
    ta_hbm,
    ca_hbm,
    em_hbm,
    pm_hbm,
    qm_hbm,
    tm_hbm,
    cm_hbm,
    sol_ref,
    hess_ref,
    blocks,
    rows_raw,
    rows_t,
    cols_side,
    trans_raw,
    coup_raw,
    trans,
    coup,
    basis,
    images,
    mixed,
    direct,
    stacked,
    a_send,
    a_slot,
    z_send,
    z_slot,
    x_send,
    x_slot,
    d_send,
    d_slot,
    c1_ref,
    c2_ref,
    c4_ref,
    c5_ref,
    bridge0,
    bridge1,
    bridge2,
    r_send,
    ra_slot,
    rz_slot,
    rx_slot,
    hs,
    load_sem,
    a_ss,
    a_rs,
    z_ss,
    z_rs,
    x_ss,
    x_rs,
    d_ss,
    d_rs,
    ra_ss,
    ra_rs,
    rz_ss,
    rz_rs,
    rx_ss,
    rx_rs,
):
    me = lax.axis_index("leaf")
    g = me % GROUP
    zc = (me // GROUP) % DEEP
    xc = me // (GROUP * DEEP)

    def to_group(k):
        return (me // GROUP) * GROUP + (g + k) % GROUP

    def to_deep(k):
        return xc * (GROUP * DEEP) + ((zc + k) % DEEP) * GROUP + g

    def to_outer(k):
        return ((xc + k) % OUTER) * (GROUP * DEEP) + me % (GROUP * DEEP)

    def load(src, dst, which):
        return pltpu.make_async_copy(src, dst, load_sem.at[which])

    loads = {
        "rhs": load(rhs_hbm, basis.at[0], 0),
        "q0": load(qm_hbm.at[0], cols_side.at[0], 1),
        "t0": load(tm_hbm, trans_raw.at[0], 2),
        "e0": load(em_hbm.at[0], blocks.at[0], 3),
        "c0": load(cm_hbm, coup_raw.at[0], 4),
        "p0": load(pm_hbm.at[0], rows_raw.at[0], 5),
        "q1": load(qa_hbm.at[0], cols_side.at[1], 6),
        "t1": load(ta_hbm, trans_raw.at[1], 7),
        "e1": load(ea_hbm.at[0], blocks.at[1], 8),
        "c1": load(ca_hbm, coup_raw.at[1], 9),
        "p1": load(pa_hbm.at[0], rows_raw.at[1], 10),
    }
    for item in loads.values():
        item.start()

    barrier = pltpu.get_barrier_semaphore()
    peers = [to_group(k) for k in range(1, GROUP)]
    peers += [to_deep(k) for k in range(1, DEEP)]
    peers += [to_outer(k) for k in range(1, OUTER)]
    for peer in peers:
        pl.semaphore_signal(barrier, inc=1, device_id=(peer,), device_id_type=MESH)

    for i in range(1, ITERS + 1):
        basis[i] = jnp.zeros((WIDTH, COLS), F32)

    def pad_tree(op):
        loads["t%d" % op].wait()
        loads["c%d" % op].wait()
        edge = ((0, LANES - RANK), (0, LANES - RANK))

        def one(h, carry):
            for s in range(2):
                trans[op, h, s * LANES : (s + 1) * LANES, :] = jnp.pad(trans_raw[op, h, s], edge)
                coup[op, h, s] = jnp.pad(coup_raw[op, h, s], edge)
            return carry

        lax.fori_loop(0, LEVELS, one, 0)

    def turn_rows(op):
        loads["p%d" % op].wait()
        for t in range(WIDTH // TILE):
            part = rows_raw[op, :, t * TILE : (t + 1) * TILE].astype(F32)
            part = jnp.pad(part, ((0, LANES - RANK), (0, 0)))
            rows_t[op, t * TILE : (t + 1) * TILE, :] = part.T.astype(BF16)

    def copies(count, coord, target, source, slot, send_sem, recv_sem):
        out = []
        arrive = []
        for k in range(1, count):
            out.append(
                pltpu.make_async_remote_copy(
                    src_ref=source(k),
                    dst_ref=slot.at[coord],
                    send_sem=send_sem.at[k - 1],
                    recv_sem=recv_sem.at[k - 1],
                    device_id=(target(k),),
                    device_id_type=MESH,
                )
            )
            arrive.append(
                pltpu.make_async_remote_copy(
                    src_ref=source(k),
                    dst_ref=slot.at[(coord + count - k) % count],
                    send_sem=send_sem.at[k - 1],
                    recv_sem=recv_sem.at[k - 1],
                    device_id=(target(k),),
                    device_id_type=MESH,
                )
            )
        return out, arrive

    def start(group):
        for c in group[0]:
            c.start()

    def arrived(group):
        for c in group[1]:
            c.wait_recv()

    def left_device(group):
        for c in group[0]:
            c.wait_send()

    def upward(x, op, h):
        left, right = pairs(x)
        joined = product_rows(
            jnp.concatenate([left, right], axis=1), trans[op, h], NN
        )
        return joined.reshape(x.shape[0] // 2, SLICE, LANES)

    def bridges(x, op, h):
        left, right = pairs(x)
        count = x.shape[0] // 2
        first = product_rows(right, coup[op, h, 0], NT).reshape(count, 1, SLICE, LANES)
        second = product_rows(left, coup[op, h, 1], NT).reshape(count, 1, SLICE, LANES)
        return jnp.concatenate([first, second], axis=1).reshape(x.shape)

    def downward(bridge, above, op, h):
        count = above.shape[0]
        moved = product_rows(above.reshape(count * SLICE, LANES), trans[op, h], NT)
        first = moved[:, :LANES].reshape(count, 1, SLICE, LANES)
        second = moved[:, LANES:].reshape(count, 1, SLICE, LANES)
        return bridge + jnp.concatenate([first, second], axis=1).reshape(bridge.shape)

    def own_bridge(values, own, op, h):
        side = own % 2
        return product_rows(values(own + 1 - 2 * side), coup[op, h, side], NT)

    def own_down(above, own, op, h):
        side = own % 2
        weight = trans[op, h, pl.ds(pl.multiple_of(side * LANES, LANES), LANES), :]
        return product_rows(above, weight, NT)

    def tree_apply(op, j, source, target):
        if op == 0:

            @pl.when(j == 0)
            def _():
                loads["rhs"].wait()

        @pl.when(j == 0)
        def _():
            loads["q%d" % op].wait()

        high, low = halves(source())
        stacked[:, :COLS] = high
        stacked[:, COLS:] = low
        both = jnp.dot(cols_side[op], stacked[...], preferred_element_type=F32)
        leaf = both[:, :COLS] + both[:, COLS:]
        leaf = jnp.pad(leaf, ((0, LANES - RANK), (0, 0)))
        a_send[op] = leaf.T.reshape(GROUP, SLICE, LANES)
        if op == 0:

            @pl.when(j == 0)
            def _():
                pl.semaphore_wait(barrier, len(peers))

        a = copies(
            GROUP, g, to_group, lambda k: a_send.at[op, (g + k) % GROUP],
            a_slot.at[op], a_ss.at[op], a_rs.at[op],
        )
        start(a)
        a_slot[op, g] = a_send[op, g]

        @pl.when(j == 0)
        def _():
            pad_tree(op)
            loads["e%d" % op].wait()

        for t in range(WIDTH // TILE):
            both = jnp.dot(
                blocks[op, t * TILE : (t + 1) * TILE, :], stacked[...],
                preferred_element_type=F32,
            )
            direct[t * TILE : (t + 1) * TILE, :] = both[:, :COLS] + both[:, COLS:]

        arrived(a)
        c1 = upward(a_slot[op], op, 0)
        c1_ref[...] = c1
        c2 = upward(c1, op, 1)
        c2_ref[...] = c2
        c3 = upward(c2, op, 2)
        z_send[op] = c3[0]
        z = copies(
            DEEP, zc, to_deep, lambda k: z_send.at[op],
            z_slot.at[op], z_ss.at[op], z_rs.at[op],
        )
        start(z)
        z_slot[op, zc] = c3[0]
        bridge0[...] = bridges(a_slot[op], op, 0)
        bridge1[...] = bridges(c1_ref[...], op, 1)
        bridge2[...] = bridges(c2_ref[...], op, 2)

        @pl.when(j == 0)
        def _():
            turn_rows(op)

        arrived(z)
        c4 = upward(z_slot[op], op, 3)
        c4_ref[...] = c4
        c5 = upward(c4, op, 4)
        c5_ref[...] = c5
        c6 = upward(c5, op, 5)
        x_send[op] = c6[0]
        x = copies(
            OUTER, xc, to_outer, lambda k: x_send.at[op],
            x_slot.at[op], x_ss.at[op], x_rs.at[op],
        )
        start(x)
        x_slot[op, xc] = c6[0]
        near3 = own_bridge(lambda n: z_slot[op, n], zc, op, 3)
        near4 = own_bridge(lambda n: c4_ref[n], zc // 2, op, 4)
        near5 = own_bridge(lambda n: c5_ref[n], zc // 4, op, 5)
        arrived(x)
        c7 = upward(x_slot[op], op, 6)
        near6 = own_bridge(lambda n: x_slot[op, n], xc, op, 6)
        c4_ref[0:2] = c7
        d7 = own_bridge(lambda n: c4_ref[n], xc // 2, op, 7)
        d6 = near6 + own_down(d7, xc, op, 6)
        d5 = near5 + own_down(d6, zc // 4, op, 5)
        d4 = near4 + own_down(d5, zc // 2, op, 4)
        d3 = near3 + own_down(d4, zc, op, 3)
        d2 = downward(bridge2[...], d3.reshape(1, SLICE, LANES), op, 2)
        d1 = downward(bridge1[...], d2, op, 1)
        d0 = downward(bridge0[...], d1, op, 0)
        d_send[op] = d0
        d = copies(
            GROUP, g, to_group, lambda k: d_send.at[op, (g + k) % GROUP],
            d_slot.at[op], d_ss.at[op], d_rs.at[op],
        )
        start(d)
        d_slot[op, g] = d_send[op, g]
        left_device(a)
        left_device(z)
        left_device(x)
        arrived(d)
        high, low = halves(d_slot[op].reshape(COLS, LANES))
        spread = jnp.concatenate([high, low], axis=0)
        for t in range(WIDTH // TILE):
            part = slice(t * TILE, (t + 1) * TILE)
            both = lax.dot_general(rows_t[op, part, :], spread, NT, preferred_element_type=F32)
            target(part, direct[part, :] + both[:, :COLS] + both[:, COLS:])
        left_device(d)

    def total_of(which, rows):
        r_send[which, 0] = rows
        ra = copies(
            GROUP, g, to_group, lambda k: r_send.at[which, 0],
            ra_slot.at[which], ra_ss.at[which], ra_rs.at[which],
        )
        start(ra)
        ra_slot[which, g] = rows
        arrived(ra)
        one = jnp.sum(ra_slot[which], axis=0)
        r_send[which, 1] = one
        rz = copies(
            DEEP, zc, to_deep, lambda k: r_send.at[which, 1],
            rz_slot.at[which], rz_ss.at[which], rz_rs.at[which],
        )
        start(rz)
        rz_slot[which, zc] = one
        arrived(rz)
        two = jnp.sum(rz_slot[which], axis=0)
        r_send[which, 2] = two
        rx = copies(
            OUTER, xc, to_outer, lambda k: r_send.at[which, 2],
            rx_slot.at[which], rx_ss.at[which], rx_rs.at[which],
        )
        start(rx)
        rx_slot[which, xc] = two
        arrived(rx)
        left_device(ra)
        left_device(rz)
        left_device(rx)
        return jnp.sum(rx_slot[which], axis=0)

    def column_sum(x):
        return jnp.sum(x, axis=0, keepdims=True)

    def iteration(j, carry):
        def to_image(part, value):
            images[j, part, :] = value

        def to_mixed(part, value):
            mixed[part, :] = value

        tree_apply(0, j, lambda: basis[j], to_image)
        tree_apply(1, j, lambda: images[j], to_mixed)
        partial = [column_sum(basis[i] * mixed[...]) for i in range(ITERS)]
        partial.append(column_sum(basis[j] * basis[j]))
        partial.append(jnp.zeros((8 - len(partial), COLS), F32))
        totals = total_of(0, jnp.concatenate(partial, axis=0))
        norm = jnp.sqrt(totals[ITERS : ITERS + 1] + EPSILON)
        hs[j * (ITERS + 1)] = norm
        scale = 1.0 / norm
        basis[j] = basis[j] * scale
        images[j] = images[j] * scale
        update = mixed[...] * scale
        for i in range(ITERS):
            entry = totals[i : i + 1] / norm
            entry = jnp.where(i == j, entry / norm, entry)
            entry = jnp.where(i > j, jnp.zeros_like(entry), entry)
            hs[j * (ITERS + 1) + 1 + i] = entry
            update = update - entry * basis[i]
        basis[j + 1] = update
        return carry

    lax.fori_loop(0, ITERS, iteration, 0)

    last = column_sum(basis[ITERS] * basis[ITERS])
    totals = total_of(1, jnp.concatenate([last, jnp.zeros((7, COLS), F32)], axis=0))
    last_norm = jnp.sqrt(totals[0:1] + EPSILON)
    zero = jnp.zeros((1, COLS), F32)
    entries = [[zero for column in range(ITERS)] for line in range(ITERS + 1)]
    for column in range(ITERS):
        for line in range(column + 1):
            entries[line][column] = hs[column * (ITERS + 1) + 1 + line]
        if column + 1 < ITERS:
            entries[column + 1][column] = hs[(column + 1) * (ITERS + 1)]
        else:
            entries[column + 1][column] = last_norm
    weights = least_squares(entries, hs[0])
    sol_ref[...] = weights[0] * images[0] + weights[1] * images[1] + weights[2] * images[2]
    for line in range(ITERS + 1):
        hess_ref[line] = jnp.concatenate(entries[line], axis=0)


def solution(mesh):
    dma = pltpu.SemaphoreType.DMA
    tree = (2, GROUP, SLICE, LANES)
    scratch = [
        pltpu.VMEM((2, WIDTH, WIDTH), BF16),
        pltpu.VMEM((2, RANK, WIDTH), BF16),
        pltpu.VMEM((2, WIDTH, LANES), BF16),
        pltpu.VMEM((2, RANK, WIDTH), BF16),
        pltpu.VMEM((2, LEVELS, 2, RANK, RANK), BF16),
        pltpu.VMEM((2, LEVELS, 2, RANK, RANK), BF16),
        pltpu.VMEM((2, LEVELS, 2 * LANES, LANES), BF16),
        pltpu.VMEM((2, LEVELS, 2, LANES, LANES), BF16),
        pltpu.VMEM((ITERS + 1, WIDTH, COLS), F32),
        pltpu.VMEM((ITERS, WIDTH, COLS), F32),
        pltpu.VMEM((WIDTH, COLS), F32),
        pltpu.VMEM((WIDTH, COLS), F32),
        pltpu.VMEM((WIDTH, 2 * COLS), BF16),
        pltpu.VMEM(tree, F32),
        pltpu.VMEM(tree, F32),
        pltpu.VMEM((2, SLICE, LANES), F32),
        pltpu.VMEM((2, DEEP, SLICE, LANES), F32),
        pltpu.VMEM((2, SLICE, LANES), F32),
        pltpu.VMEM((2, OUTER, SLICE, LANES), F32),
        pltpu.VMEM(tree, F32),
        pltpu.VMEM(tree, F32),
        pltpu.VMEM((4, SLICE, LANES), F32),
        pltpu.VMEM((2, SLICE, LANES), F32),
        pltpu.VMEM((4, SLICE, LANES), F32),
        pltpu.VMEM((2, SLICE, LANES), F32),
        pltpu.VMEM((8, SLICE, LANES), F32),
        pltpu.VMEM((4, SLICE, LANES), F32),
        pltpu.VMEM((2, SLICE, LANES), F32),
        pltpu.VMEM((2, 3, 8, COLS), F32),
        pltpu.VMEM((2, GROUP, 8, COLS), F32),
        pltpu.VMEM((2, DEEP, 8, COLS), F32),
        pltpu.VMEM((2, OUTER, 8, COLS), F32),
        pltpu.VMEM((ITERS * (ITERS + 1), 1, COLS), F32),
        dma((11,)),
        dma((2, GROUP - 1)),
        dma((2, GROUP - 1)),
        dma((2, DEEP - 1)),
        dma((2, DEEP - 1)),
        dma((2, OUTER - 1)),
        dma((2, OUTER - 1)),
        dma((2, GROUP - 1)),
        dma((2, GROUP - 1)),
        dma((2, GROUP - 1)),
        dma((2, GROUP - 1)),
        dma((2, DEEP - 1)),
        dma((2, DEEP - 1)),
        dma((2, OUTER - 1)),
        dma((2, OUTER - 1)),
    ]

    def on_device(*args):
        return pl.pallas_call(
            kernel,
            out_shape=(
                jax.ShapeDtypeStruct((WIDTH, COLS), F32),
                jax.ShapeDtypeStruct((ITERS + 1, ITERS, COLS), F32),
            ),
            in_specs=[pl.BlockSpec(memory_space=pl.ANY)] * 11,
            out_specs=[pl.BlockSpec(memory_space=pltpu.VMEM)] * 2,
            scratch_shapes=scratch,
            compiler_params=pltpu.CompilerParams(
                collective_id=0, has_side_effects=True, vmem_limit_bytes=60 * 2**20
            ),
        )(*args)

    leaf = P("leaf", None)
    block = P("leaf", None, None)
    in_specs = (leaf, block, block, block, P(), P(), block, block, block, P(), P())
    return jax.shard_map(
        on_device, mesh=mesh, in_specs=in_specs, out_specs=(leaf, P()), check_vma=False
    )
```

time: 536 us -> 188 us (0.35); the launches traced: 527 us -> 188 us
  Pallas kernels: 0 us -> 184 us
  blocking collectives: 173 us -> 0 us
  waiting for transfers between devices: 167 us -> 0 us
  matrix products: 94.4 us -> 0 us
  starting transfers between devices: 73.4 us -> 0 us
  other arithmetic: 8.21 us -> 0 us
    pallas_call x0 -> x1, Pallas kernels: none -> 184 us  [on_device(): pl.pallas_call(kernel, out_shape=(jax.ShapeDtypeStruct((WIDTH, COLS), F32...]
    psum x16 -> x0, blocking collectives: 173 us -> none  [over_axes(): return functools.reduce(lax.psum, axes, x)]
    ppermute x48 -> x0, waiting for transfers between devices: 167 us -> none  [from_partner(): return lax.ppermute(block, axis, route)]
    dot_general x192 -> x0, matrix products: 94.4 us -> none  [the longest x90 44.6 us: transpose_apply(): lax.dot_general(matrix, vectors, (((0,), (0,)), ((), ())), precision=lax....]
    ppermute x48 -> x0, starting transfers between devices: 73.4 us -> none  [from_partner(): return lax.ppermute(block, axis, route)]
  transfers between devices with their start and end apart: 48 -> 0, of which waited for: 46 -> 0; matrix products, arithmetic and copies ran while one was open for 2% -> 0% of each run, Pallas kernels for 0% -> 0%
where the time goes in v1:
time: 188 us
  Pallas kernels  184 us (98%)
  local copies, waits for them, and re-layouts  3.16 us (2%)
    pallas_call x1, Pallas kernels, on_device(): pl.pallas_call(kernel, out_shape=(jax.ShapeDtypeStruct((WIDTH, COLS), F32...  184 us

profile of v1, /device:TPU:1, one launch (start us, length us, event | category | flops | bytes accessed | tf_op | source)
XLA Modules:
  0.0 188.0 jit_solution(1328699485631450412)
XLA Ops:
  0.6 184.2 %shard_map.122 = (f32[1024,128]{1,0:T(8,128)}, f32[4,3,128]{2,1,0:T(4,128)}) custom-call(f32[1024,128]{1,0:T(8,128)} %rhs_hbm.1, bf16[1,1024,1024]{2,1,0:T(8,128)(2,1)} %ea_hbm.1, bf16[1,200,1024]{2,1,0:T(8,128)(2,1)} %pa_hbm.1, bf16[1,200,1024]{2,1,0:T(8,128)(2,1)} %qa_hbm.1, bf16[8,2,200,200]{3,2,1,0:T(8,128)(2,1)} %ta_hbm.1, ...), custom_call_target="tpu_custom_call" | custom-call | tf_op jit(solution)/shard_map/pallas_call | solution.py:522
  184.8 1.3 copy.13
  186.1 1.9 copy.15

commit v2 on v1

--- a/solution.py
+++ b/solution.py
@@ -157,7 +157,7 @@
         return pltpu.make_async_copy(src, dst, load_sem.at[which])
 
     loads = {
-        "rhs": load(rhs_hbm, basis.at[0], 0),
+        "rhs": load(rhs_hbm, mixed, 0),
         "q0": load(qm_hbm.at[0], cols_side.at[0], 1),
         "t0": load(tm_hbm, trans_raw.at[0], 2),
         "e0": load(em_hbm.at[0], blocks.at[0], 3),
@@ -179,8 +179,9 @@
     for peer in peers:
         pl.semaphore_signal(barrier, inc=1, device_id=(peer,), device_id_type=MESH)
 
-    for i in range(1, ITERS + 1):
+    for i in range(1, ITERS):
         basis[i] = jnp.zeros((WIDTH, COLS), F32)
+        images[i] = jnp.zeros((WIDTH, COLS), F32)
 
     def pad_tree(op):
         loads["t%d" % op].wait()
@@ -270,12 +271,19 @@
         weight = trans[op, h, pl.ds(pl.multiple_of(side * LANES, LANES), LANES), :]
         return product_rows(above, weight, NT)
 
-    def tree_apply(op, j, source, target):
+    def riding(x):
+        lane = lax.broadcasted_iota(jnp.int32, (SLICE, LANES - COLS), 1)
+        total = jnp.sum(x[:, :, COLS:], axis=0)
+        total = jnp.where(lane >= RANK - COLS, total, jnp.zeros_like(total))
+        return jnp.concatenate([jnp.zeros((SLICE, COLS), F32), total], axis=1)
+
+    def tree_apply(op, j, source, target, sums=None):
         if op == 0:
 
             @pl.when(j == 0)
             def _():
                 loads["rhs"].wait()
+                basis[0] = mixed[...]
 
         @pl.when(j == 0)
         def _():
@@ -286,7 +294,12 @@
         stacked[:, COLS:] = low
         both = jnp.dot(cols_side[op], stacked[...], preferred_element_type=F32)
         leaf = both[:, :COLS] + both[:, COLS:]
-        leaf = jnp.pad(leaf, ((0, LANES - RANK), (0, 0)))
+        rest = LANES - RANK
+        if sums is None:
+            leaf = jnp.pad(leaf, ((0, rest), (0, 0)))
+        else:
+            pad = jnp.zeros((rest - 8, COLS), F32)
+            leaf = jnp.concatenate([leaf, sums(), pad], axis=0)
         a_send[op] = leaf.T.reshape(GROUP, SLICE, LANES)
         if op == 0:
 
@@ -319,13 +332,14 @@
         c2 = upward(c1, op, 1)
         c2_ref[...] = c2
         c3 = upward(c2, op, 2)
-        z_send[op] = c3[0]
+        c3 = c3[0] if sums is None else c3[0] + riding(a_slot[op])
+        z_send[op] = c3
         z = copies(
             DEEP, zc, to_deep, lambda k: z_send.at[op],
             z_slot.at[op], z_ss.at[op], z_rs.at[op],
         )
         start(z)
-        z_slot[op, zc] = c3[0]
+        z_slot[op, zc] = c3
         bridge0[...] = bridges(a_slot[op], op, 0)
         bridge1[...] = bridges(c1_ref[...], op, 1)
         bridge2[...] = bridges(c2_ref[...], op, 2)
@@ -340,13 +354,14 @@
         c5 = upward(c4, op, 4)
         c5_ref[...] = c5
         c6 = upward(c5, op, 5)
-        x_send[op] = c6[0]
+        c6 = c6[0] if sums is None else c6[0] + riding(z_slot[op])
+        x_send[op] = c6
         x = copies(
             OUTER, xc, to_outer, lambda k: x_send.at[op],
             x_slot.at[op], x_ss.at[op], x_rs.at[op],
         )
         start(x)
-        x_slot[op, xc] = c6[0]
+        x_slot[op, xc] = c6
         near3 = own_bridge(lambda n: z_slot[op, n], zc, op, 3)
         near4 = own_bridge(lambda n: c4_ref[n], zc // 2, op, 4)
         near5 = own_bridge(lambda n: c5_ref[n], zc // 4, op, 5)
@@ -362,7 +377,7 @@
         d2 = downward(bridge2[...], d3.reshape(1, SLICE, LANES), op, 2)
         d1 = downward(bridge1[...], d2, op, 1)
         d0 = downward(bridge0[...], d1, op, 0)
-        d_send[op] = d0
+        d_send[op] = d0 if sums is None else d0 + riding(x_slot[op])[None]
         d = copies(
             GROUP, g, to_group, lambda k: d_send.at[op, (g + k) % GROUP],
             d_slot.at[op], d_ss.at[op], d_rs.at[op],
@@ -375,11 +390,15 @@
         arrived(d)
         high, low = halves(d_slot[op].reshape(COLS, LANES))
         spread = jnp.concatenate([high, low], axis=0)
+        totals = None
+        if sums is not None:
+            totals = d_slot[op].reshape(COLS, LANES)[:, COLS:].T[RANK - COLS : RANK - COLS + 8]
         for t in range(WIDTH // TILE):
             part = slice(t * TILE, (t + 1) * TILE)
             both = lax.dot_general(rows_t[op, part, :], spread, NT, preferred_element_type=F32)
             target(part, direct[part, :] + both[:, :COLS] + both[:, COLS:])
         left_device(d)
+        return totals
 
     def total_of(which, rows):
         r_send[which, 0] = rows
@@ -416,37 +435,62 @@
     def column_sum(x):
         return jnp.sum(x, axis=0, keepdims=True)
 
-    def iteration(j, carry):
-        def to_image(part, value):
-            images[j, part, :] = value
-
-        def to_mixed(part, value):
-            mixed[part, :] = value
-
-        tree_apply(0, j, lambda: basis[j], to_image)
-        tree_apply(1, j, lambda: images[j], to_mixed)
-        partial = [column_sum(basis[i] * mixed[...]) for i in range(ITERS)]
-        partial.append(column_sum(basis[j] * basis[j]))
-        partial.append(jnp.zeros((8 - len(partial), COLS), F32))
-        totals = total_of(0, jnp.concatenate(partial, axis=0))
+    def partial_sums(j):
+        rows = [column_sum(basis[i] * mixed[...]) for i in range(ITERS)]
+        rows.append(column_sum(basis[j] * basis[j]))
+        rows.append(jnp.zeros((8 - len(rows), COLS), F32))
+        return jnp.concatenate(rows, axis=0)
+
+    def arnoldi_column(totals, j):
         norm = jnp.sqrt(totals[ITERS : ITERS + 1] + EPSILON)
         hs[j * (ITERS + 1)] = norm
-        scale = 1.0 / norm
-        basis[j] = basis[j] * scale
-        images[j] = images[j] * scale
-        update = mixed[...] * scale
+        entries = []
         for i in range(ITERS):
             entry = totals[i : i + 1] / norm
             entry = jnp.where(i == j, entry / norm, entry)
             entry = jnp.where(i > j, jnp.zeros_like(entry), entry)
             hs[j * (ITERS + 1) + 1 + i] = entry
-            update = update - entry * basis[i]
-        basis[j + 1] = update
+            entries.append(entry)
+        return 1.0 / norm, entries
+
+    def iteration(j, carry):
+        def to_image(part, value):
+            images[j, part, :] = value
+
+        def to_mixed(part, value):
+            mixed[part, :] = value
+
+        before = jnp.maximum(j - 1, 0)
+        totals = tree_apply(0, j, lambda: mixed[...], to_image, lambda: partial_sums(before))
+
+        @pl.when(j > 0)
+        def _():
+            scale, entries = arnoldi_column(totals, before)
+            for t in range(WIDTH // TILE):
+                part = slice(t * TILE, (t + 1) * TILE)
+                basis[before, part, :] = basis[before, part, :] * scale
+                images[before, part, :] = images[before, part, :] * scale
+                image = images[j, part, :] * scale
+                update = mixed[part, :] * scale
+                for i in range(ITERS - 1):
+                    image = image - entries[i] * images[i, part, :]
+                    update = update - entries[i] * basis[i, part, :]
+                images[j, part, :] = image
+                basis[j, part, :] = update
+
+        tree_apply(1, j, lambda: images[j], to_mixed)
         return carry
 
     lax.fori_loop(0, ITERS, iteration, 0)
 
-    last = column_sum(basis[ITERS] * basis[ITERS])
+    totals = total_of(0, partial_sums(ITERS - 1))
+    scale, entries = arnoldi_column(totals, ITERS - 1)
+    basis[ITERS - 1] = basis[ITERS - 1] * scale
+    images[ITERS - 1] = images[ITERS - 1] * scale
+    update = mixed[...] * scale
+    for i in range(ITERS):
+        update = update - entries[i] * basis[i]
+    last = column_sum(update * update)
     totals = total_of(1, jnp.concatenate([last, jnp.zeros((7, COLS), F32)], axis=0))
     last_norm = jnp.sqrt(totals[0:1] + EPSILON)
     zero = jnp.zeros((1, COLS), F32)
@@ -476,7 +520,7 @@
         pltpu.VMEM((2, LEVELS, 2, RANK, RANK), BF16),
         pltpu.VMEM((2, LEVELS, 2 * LANES, LANES), BF16),
         pltpu.VMEM((2, LEVELS, 2, LANES, LANES), BF16),
-        pltpu.VMEM((ITERS + 1, WIDTH, COLS), F32),
+        pltpu.VMEM((ITERS, WIDTH, COLS), F32),
         pltpu.VMEM((ITERS, WIDTH, COLS), F32),
         pltpu.VMEM((WIDTH, COLS), F32),
         pltpu.VMEM((WIDTH, COLS), F32),

time: 188 us -> 165 us (0.88)
  Pallas kernels: 184 us -> 161 us
    pallas_call x1, Pallas kernels: 184 us -> 161 us  [on_device(): pl.pallas_call(kernel, out_shape=(jax.ShapeDtypeStruct((WIDTH, COLS), F32...]
where the time goes in v2:
time: 165 us
  Pallas kernels  161 us (98%)
  local copies, waits for them, and re-layouts  3.16 us (2%)
    pallas_call x1, Pallas kernels, on_device(): pl.pallas_call(kernel, out_shape=(jax.ShapeDtypeStruct((WIDTH, COLS), F32...  161 us

profile of v2, /device:TPU:1, one launch (start us, length us, event | category | flops | bytes accessed | tf_op | source)
XLA Modules:
  0.0 164.6 jit_solution(6167325159927499558)
XLA Ops:
  0.6 160.8 %shard_map.122 = (f32[1024,128]{1,0:T(8,128)}, f32[4,3,128]{2,1,0:T(4,128)}) custom-call(f32[1024,128]{1,0:T(8,128)} %rhs_hbm.1, bf16[1,1024,1024]{2,1,0:T(8,128)(2,1)} %ea_hbm.1, bf16[1,200,1024]{2,1,0:T(8,128)(2,1)} %pa_hbm.1, bf16[1,200,1024]{2,1,0:T(8,128)(2,1)} %qa_hbm.1, bf16[8,2,200,200]{3,2,1,0:T(8,128)(2,1)} %ta_hbm.1, ...), custom_call_target="tpu_custom_call" | custom-call | tf_op jit(solution)/shard_map/pallas_call | solution.py:566
  161.5 1.3 copy.13
  162.7 1.9 %copy.15 = f32[1024,128]{1,0:T(8,128)} copy(f32[1024,128]{1,0:T(8,128)} %get-tuple-element.6) | data formatting | bytes 1048576

commit v3 on v2

--- a/solution.py
+++ b/solution.py
@@ -123,6 +123,10 @@
     rz_slot,
     rx_slot,
     hs,
+    joins,
+    join_w,
+    carried,
+    fresh,
     load_sem,
     a_ss,
     a_rs,
@@ -138,6 +142,8 @@
     rz_rs,
     rx_ss,
     rx_rs,
+    j_ss,
+    j_rs,
 ):
     me = lax.axis_index("leaf")
     g = me % GROUP
@@ -182,6 +188,7 @@
     for i in range(1, ITERS):
         basis[i] = jnp.zeros((WIDTH, COLS), F32)
         images[i] = jnp.zeros((WIDTH, COLS), F32)
+        carried[i] = jnp.zeros((GROUP, SLICE, LANES), F32)
 
     def pad_tree(op):
         loads["t%d" % op].wait()
@@ -197,7 +204,6 @@
         lax.fori_loop(0, LEVELS, one, 0)
 
     def turn_rows(op):
-        loads["p%d" % op].wait()
         for t in range(WIDTH // TILE):
             part = rows_raw[op, :, t * TILE : (t + 1) * TILE].astype(F32)
             part = jnp.pad(part, ((0, LANES - RANK), (0, 0)))
@@ -277,19 +283,8 @@
         total = jnp.where(lane >= RANK - COLS, total, jnp.zeros_like(total))
         return jnp.concatenate([jnp.zeros((SLICE, COLS), F32), total], axis=1)
 
-    def tree_apply(op, j, source, target, sums=None):
-        if op == 0:
-
-            @pl.when(j == 0)
-            def _():
-                loads["rhs"].wait()
-                basis[0] = mixed[...]
-
-        @pl.when(j == 0)
-        def _():
-            loads["q%d" % op].wait()
-
-        high, low = halves(source())
+    def leaf_terms(op, value, sums=None):
+        high, low = halves(value)
         stacked[:, :COLS] = high
         stacked[:, COLS:] = low
         both = jnp.dot(cols_side[op], stacked[...], preferred_element_type=F32)
@@ -299,26 +294,29 @@
             leaf = jnp.pad(leaf, ((0, rest), (0, 0)))
         else:
             pad = jnp.zeros((rest - 8, COLS), F32)
-            leaf = jnp.concatenate([leaf, sums(), pad], axis=0)
+            leaf = jnp.concatenate([leaf, sums, pad], axis=0)
         a_send[op] = leaf.T.reshape(GROUP, SLICE, LANES)
-        if op == 0:
-
-            @pl.when(j == 0)
-            def _():
-                pl.semaphore_wait(barrier, len(peers))
-
+
+    def send_leaf(op):
         a = copies(
             GROUP, g, to_group, lambda k: a_send.at[op, (g + k) % GROUP],
             a_slot.at[op], a_ss.at[op], a_rs.at[op],
         )
         start(a)
         a_slot[op, g] = a_send[op, g]
-
-        @pl.when(j == 0)
-        def _():
-            pad_tree(op)
-            loads["e%d" % op].wait()
-
+        return a
+
+    def send_down(op, value):
+        d_send[op] = value
+        d = copies(
+            GROUP, g, to_group, lambda k: d_send.at[op, (g + k) % GROUP],
+            d_slot.at[op], d_ss.at[op], d_rs.at[op],
+        )
+        start(d)
+        d_slot[op, g] = d_send[op, g]
+        return d
+
+    def block_product(op):
         for t in range(WIDTH // TILE):
             both = jnp.dot(
                 blocks[op, t * TILE : (t + 1) * TILE, :], stacked[...],
@@ -326,13 +324,21 @@
             )
             direct[t * TILE : (t + 1) * TILE, :] = both[:, :COLS] + both[:, COLS:]
 
-        arrived(a)
-        c1 = upward(a_slot[op], op, 0)
+    def spread_down(op, target):
+        high, low = halves(d_slot[op].reshape(COLS, LANES))
+        spread = jnp.concatenate([high, low], axis=0)
+        for t in range(WIDTH // TILE):
+            part = slice(t * TILE, (t + 1) * TILE)
+            both = lax.dot_general(rows_t[op, part, :], spread, NT, preferred_element_type=F32)
+            target(part, direct[part, :] + both[:, :COLS] + both[:, COLS:])
+
+    def tree(op, leaves, sums, while_z=None, while_x=None):
+        c1 = upward(leaves(), op, 0)
         c1_ref[...] = c1
         c2 = upward(c1, op, 1)
         c2_ref[...] = c2
         c3 = upward(c2, op, 2)
-        c3 = c3[0] if sums is None else c3[0] + riding(a_slot[op])
+        c3 = c3[0] + riding(leaves()) if sums else c3[0]
         z_send[op] = c3
         z = copies(
             DEEP, zc, to_deep, lambda k: z_send.at[op],
@@ -340,21 +346,18 @@
         )
         start(z)
         z_slot[op, zc] = c3
-        bridge0[...] = bridges(a_slot[op], op, 0)
+        bridge0[...] = bridges(leaves(), op, 0)
         bridge1[...] = bridges(c1_ref[...], op, 1)
         bridge2[...] = bridges(c2_ref[...], op, 2)
-
-        @pl.when(j == 0)
-        def _():
-            turn_rows(op)
-
+        if while_z is not None:
+            while_z()
         arrived(z)
         c4 = upward(z_slot[op], op, 3)
         c4_ref[...] = c4
         c5 = upward(c4, op, 4)
         c5_ref[...] = c5
         c6 = upward(c5, op, 5)
-        c6 = c6[0] if sums is None else c6[0] + riding(z_slot[op])
+        c6 = c6[0] + riding(z_slot[op]) if sums else c6[0]
         x_send[op] = c6
         x = copies(
             OUTER, xc, to_outer, lambda k: x_send.at[op],
@@ -365,6 +368,8 @@
         near3 = own_bridge(lambda n: z_slot[op, n], zc, op, 3)
         near4 = own_bridge(lambda n: c4_ref[n], zc // 2, op, 4)
         near5 = own_bridge(lambda n: c5_ref[n], zc // 4, op, 5)
+        if while_x is not None:
+            while_x()
         arrived(x)
         c7 = upward(x_slot[op], op, 6)
         near6 = own_bridge(lambda n: x_slot[op, n], xc, op, 6)
@@ -377,28 +382,77 @@
         d2 = downward(bridge2[...], d3.reshape(1, SLICE, LANES), op, 2)
         d1 = downward(bridge1[...], d2, op, 1)
         d0 = downward(bridge0[...], d1, op, 0)
-        d_send[op] = d0 if sums is None else d0 + riding(x_slot[op])[None]
-        d = copies(
-            GROUP, g, to_group, lambda k: d_send.at[op, (g + k) % GROUP],
-            d_slot.at[op], d_ss.at[op], d_rs.at[op],
-        )
-        start(d)
-        d_slot[op, g] = d_send[op, g]
-        left_device(a)
         left_device(z)
         left_device(x)
-        arrived(d)
-        high, low = halves(d_slot[op].reshape(COLS, LANES))
-        spread = jnp.concatenate([high, low], axis=0)
-        totals = None
-        if sums is not None:
-            totals = d_slot[op].reshape(COLS, LANES)[:, COLS:].T[RANK - COLS : RANK - COLS + 8]
-        for t in range(WIDTH // TILE):
-            part = slice(t * TILE, (t + 1) * TILE)
-            both = lax.dot_general(rows_t[op, part, :], spread, NT, preferred_element_type=F32)
-            target(part, direct[part, :] + both[:, :COLS] + both[:, COLS:])
-        left_device(d)
-        return totals
+        return d0
+
+    partner = g + 1 - 2 * (g % 2)
+    join_out = []
+    join_in = []
+    for k in range(4):
+        to = to_group(2 * k) if k else (me // GROUP) * GROUP + partner
+        source = (g + GROUP - 2 * k) % GROUP if k else partner
+        for group, where in ((join_out, g), (join_in, source)):
+            group.append(
+                pltpu.make_async_remote_copy(
+                    src_ref=joins.at[g], dst_ref=joins.at[where],
+                    send_sem=j_ss.at[k], recv_sem=j_rs.at[k],
+                    device_id=(to,), device_id_type=MESH,
+                )
+            )
+    pass_out = []
+    pass_in = []
+    for k in range(1, 4):
+        mine = (g + GROUP - 2 * k) % GROUP
+        theirs = (partner + GROUP - 2 * k) % GROUP
+        for group, where in ((pass_out, mine), (pass_in, theirs)):
+            group.append(
+                pltpu.make_async_remote_copy(
+                    src_ref=joins.at[mine], dst_ref=joins.at[where],
+                    send_sem=j_ss.at[3 + k], recv_sem=j_rs.at[3 + k],
+                    device_id=((me // GROUP) * GROUP + partner,), device_id_type=MESH,
+                )
+            )
+
+    def begin_joins():
+        loads["p0"].wait()
+        loads["q1"].wait()
+        own = lax.dot_general(rows_raw[0], cols_side[1], NT, preferred_element_type=F32)
+        joins[g] = jnp.pad(own, ((0, 0), (0, LANES - RANK)))
+        for c in join_out:
+            c.start()
+        turn_rows(0)
+
+    def pass_joins():
+        loads["p1"].wait()
+        turn_rows(1)
+        for k in range(1, 4):
+            join_in[k].wait_recv()
+            pass_out[k - 1].start()
+
+    def end_joins():
+        join_in[0].wait_recv()
+        for c in pass_in:
+            c.wait_recv()
+
+        def one(i, carry):
+            high, low = halves(jnp.pad(joins[i], ((0, LANES - RANK), (0, 0))))
+            join_w[i, 0] = high
+            join_w[i, 1] = low
+            return carry
+
+        lax.fori_loop(0, GROUP, one, 0)
+        for c in join_out + pass_out:
+            c.wait_send()
+
+    def joined_rows(x, i):
+        high, low = halves(x)
+        main = jnp.dot(
+            jnp.concatenate([high, low], axis=0), join_w[i, 0], preferred_element_type=F32
+        )
+        return main[:SLICE] + main[SLICE:] + jnp.dot(
+            high, join_w[i, 1], preferred_element_type=F32
+        )
 
     def total_of(which, rows):
         r_send[which, 0] = rows
@@ -441,47 +495,124 @@
         rows.append(jnp.zeros((8 - len(rows), COLS), F32))
         return jnp.concatenate(rows, axis=0)
 
-    def arnoldi_column(totals, j):
-        norm = jnp.sqrt(totals[ITERS : ITERS + 1] + EPSILON)
-        hs[j * (ITERS + 1)] = norm
+    def column_entries(sums, j):
+        norm = jnp.sqrt(sums(ITERS) + EPSILON)
         entries = []
         for i in range(ITERS):
-            entry = totals[i : i + 1] / norm
+            entry = sums(i) / norm
             entry = jnp.where(i == j, entry / norm, entry)
-            entry = jnp.where(i > j, jnp.zeros_like(entry), entry)
-            hs[j * (ITERS + 1) + 1 + i] = entry
-            entries.append(entry)
-        return 1.0 / norm, entries
+            entries.append(jnp.where(i > j, jnp.zeros_like(entry), entry))
+        return norm, 1.0 / norm, entries
+
+    def arnoldi_column(totals, j):
+        norm, scale, entries = column_entries(lambda i: totals[i : i + 1], j)
+        hs[j * (ITERS + 1)] = norm
+        for i in range(ITERS):
+            hs[j * (ITERS + 1) + 1 + i] = entries[i]
+        return scale, entries
+
+    def to_mixed(part, value):
+        mixed[part, :] = value
+
+    def first():
+        loads["rhs"].wait()
+        loads["q0"].wait()
+        basis[0] = mixed[...]
+        leaf_terms(0, mixed[...])
+        pl.semaphore_wait(barrier, len(peers))
+        a = send_leaf(0)
+        pad_tree(0)
+        loads["e0"].wait()
+        block_product(0)
+        arrived(a)
+        low = tree(0, lambda: a_slot[0], False, while_z=begin_joins)
+        d = send_down(0, low)
+        left_device(a)
+        pad_tree(1)
+        arrived(d)
+
+        def to_image(part, value):
+            images[0, part, :] = value
+
+        spread_down(0, to_image)
+        left_device(d)
+        leaf_terms(1, images[0])
+        a = send_leaf(1)
+        loads["e1"].wait()
+        block_product(1)
+        arrived(a)
+        carried[0] = a_slot[1]
+        low = tree(1, lambda: carried[0], False, while_z=pass_joins)
+        d = send_down(1, low)
+        left_device(a)
+        arrived(d)
+        spread_down(1, to_mixed)
+        left_device(d)
 
     def iteration(j, carry):
-        def to_image(part, value):
-            images[j, part, :] = value
-
-        def to_mixed(part, value):
-            mixed[part, :] = value
-
-        before = jnp.maximum(j - 1, 0)
-        totals = tree_apply(0, j, lambda: mixed[...], to_image, lambda: partial_sums(before))
-
-        @pl.when(j > 0)
-        def _():
+        before = j - 1
+        leaf_terms(0, mixed[...], partial_sums(before))
+        a0 = send_leaf(0)
+        block_product(0)
+        leaf_terms(1, direct[...])
+        a1 = send_leaf(1)
+        arrived(a0)
+
+        def weights_ready():
+            @pl.when(j == 1)
+            def _():
+                end_joins()
+
+        low = tree(0, lambda: a_slot[0], True, while_z=weights_ready)
+        d = send_down(0, low + riding(x_slot[0])[None])
+
+        arrived(a1)
+        sums = jnp.sum(x_slot[0, :, :, COLS:], axis=0)
+        norm, scale, entries = column_entries(
+            lambda i: sums[:, RANK - COLS + i : RANK - COLS + i + 1], before
+        )
+        carried[before] = carried[before] * scale[None]
+        for i in range(GROUP):
+            value = (a_slot[1, i] + joined_rows(low[i], i)) * scale
+            for earlier in range(ITERS - 1):
+                value = value - entries[earlier] * carried[earlier, i]
+            fresh[i] = value
+        carried[j] = fresh[...]
+        left_device(a0)
+        left_device(a1)
+
+        def orthogonalise():
+            arrived(d)
+            totals = d_slot[0].reshape(COLS, LANES)[:, COLS:].T[RANK - COLS : RANK - COLS + 8]
             scale, entries = arnoldi_column(totals, before)
-            for t in range(WIDTH // TILE):
-                part = slice(t * TILE, (t + 1) * TILE)
-                basis[before, part, :] = basis[before, part, :] * scale
-                images[before, part, :] = images[before, part, :] * scale
-                image = images[j, part, :] * scale
+            basis[before] = basis[before] * scale
+            images[before] = images[before] * scale
+
+            def finish(part, image):
+                image = image * scale
                 update = mixed[part, :] * scale
                 for i in range(ITERS - 1):
                     image = image - entries[i] * images[i, part, :]
                     update = update - entries[i] * basis[i, part, :]
                 images[j, part, :] = image
                 basis[j, part, :] = update
-
-        tree_apply(1, j, lambda: images[j], to_mixed)
+                high, low = halves(image)
+                stacked[part, :COLS] = high
+                stacked[part, COLS:] = low
+
+            spread_down(0, finish)
+
+        low = tree(1, lambda: fresh[...], False, while_x=orthogonalise)
+        e = send_down(1, low)
+        block_product(1)
+        left_device(d)
+        arrived(e)
+        spread_down(1, to_mixed)
+        left_device(e)
         return carry
 
-    lax.fori_loop(0, ITERS, iteration, 0)
+    first()
+    lax.fori_loop(1, ITERS, iteration, 0)
 
     totals = total_of(0, partial_sums(ITERS - 1))
     scale, entries = arnoldi_column(totals, ITERS - 1)
@@ -545,6 +676,10 @@
         pltpu.VMEM((2, DEEP, 8, COLS), F32),
         pltpu.VMEM((2, OUTER, 8, COLS), F32),
         pltpu.VMEM((ITERS * (ITERS + 1), 1, COLS), F32),
+        pltpu.VMEM((GROUP, RANK, LANES), F32),
+        pltpu.VMEM((GROUP, 2, LANES, LANES), BF16),
+        pltpu.VMEM((ITERS,) + tree[1:], F32),
+        pltpu.VMEM(tree[1:], F32),
         dma((11,)),
         dma((2, GROUP - 1)),
         dma((2, GROUP - 1)),
@@ -560,6 +695,8 @@
         dma((2, DEEP - 1)),
         dma((2, OUTER - 1)),
         dma((2, OUTER - 1)),
+        dma((7,)),
+        dma((7,)),
     ]
 
     def on_device(*args):

time: 165 us -> 148 us (0.90)
  Pallas kernels: 161 us -> 144 us
    pallas_call x1, Pallas kernels: 161 us -> 144 us  [on_device(): pl.pallas_call(kernel, out_shape=(jax.ShapeDtypeStruct((WIDTH, COLS), F32...]
where the time goes in v3:
time: 148 us; the launch traced here: 147 us
  Pallas kernels  144 us (97%)
  local copies, waits for them, and re-layouts  3.16 us (2%)
    pallas_call x1, Pallas kernels, on_device(): pl.pallas_call(kernel, out_shape=(jax.ShapeDtypeStruct((WIDTH, COLS), F32...  144 us

profile of v3, /device:TPU:1, one launch (start us, length us, event | category | flops | bytes accessed | tf_op | source)
XLA Modules:
  0.0 147.4 jit_solution(12500141571770787284)
XLA Ops:
  0.6 143.6 %shard_map.122 = (f32[1024,128]{1,0:T(8,128)}, f32[4,3,128]{2,1,0:T(4,128)}) custom-call(f32[1024,128]{1,0:T(8,128)} %rhs_hbm.1, bf16[1,1024,1024]{2,1,0:T(8,128)(2,1)} %ea_hbm.1, bf16[1,200,1024]{2,1,0:T(8,128)(2,1)} %pa_hbm.1, bf16[1,200,1024]{2,1,0:T(8,128)(2,1)} %qa_hbm.1, bf16[8,2,200,200]{3,2,1,0:T(8,128)(2,1)} %ta_hbm.1, ...), custom_call_target="tpu_custom_call" | custom-call | tf_op jit(solution)/shard_map/pallas_call | solution.py:703
  144.3 1.3 copy.13
  145.6 1.9 %copy.15 = f32[1024,128]{1,0:T(8,128)} copy(f32[1024,128]{1,0:T(8,128)} %get-tuple-element.6) | data formatting | bytes 1048576

commit v4 on v3

--- a/solution.py
+++ b/solution.py
@@ -123,6 +123,7 @@
     rz_slot,
     rx_slot,
     hs,
+    sums_ref,
     joins,
     join_w,
     carried,
@@ -165,11 +166,11 @@
     loads = {
         "rhs": load(rhs_hbm, mixed, 0),
         "q0": load(qm_hbm.at[0], cols_side.at[0], 1),
+        "p0": load(pm_hbm.at[0], rows_raw.at[0], 5),
+        "q1": load(qa_hbm.at[0], cols_side.at[1], 6),
         "t0": load(tm_hbm, trans_raw.at[0], 2),
         "e0": load(em_hbm.at[0], blocks.at[0], 3),
         "c0": load(cm_hbm, coup_raw.at[0], 4),
-        "p0": load(pm_hbm.at[0], rows_raw.at[0], 5),
-        "q1": load(qa_hbm.at[0], cols_side.at[1], 6),
         "t1": load(ta_hbm, trans_raw.at[1], 7),
         "e1": load(ea_hbm.at[0], blocks.at[1], 8),
         "c1": load(ca_hbm, coup_raw.at[1], 9),
@@ -185,7 +186,8 @@
     for peer in peers:
         pl.semaphore_signal(barrier, inc=1, device_id=(peer,), device_id_type=MESH)
 
-    for i in range(1, ITERS):
+    sums_ref[...] = jnp.zeros((8, COLS), F32)
+    for i in range(ITERS):
         basis[i] = jnp.zeros((WIDTH, COLS), F32)
         images[i] = jnp.zeros((WIDTH, COLS), F32)
         carried[i] = jnp.zeros((GROUP, SLICE, LANES), F32)
@@ -236,8 +238,9 @@
         return out, arrive
 
     def start(group):
-        for c in group[0]:
-            c.start()
+        count = len(group[0]) + 1
+        for k in sorted(range(1, count), key=lambda k: -min(k, count - k)):
+            group[0][k - 1].start()
 
     def arrived(group):
         for c in group[1]:
@@ -421,11 +424,8 @@
         joins[g] = jnp.pad(own, ((0, 0), (0, LANES - RANK)))
         for c in join_out:
             c.start()
-        turn_rows(0)
 
     def pass_joins():
-        loads["p1"].wait()
-        turn_rows(1)
         for k in range(1, 4):
             join_in[k].wait_recv()
             pass_out[k - 1].start()
@@ -506,71 +506,51 @@
 
     def arnoldi_column(totals, j):
         norm, scale, entries = column_entries(lambda i: totals[i : i + 1], j)
-        hs[j * (ITERS + 1)] = norm
+        place = jnp.maximum(j, 0) * (ITERS + 1)
+        hs[place] = norm
         for i in range(ITERS):
-            hs[j * (ITERS + 1) + 1 + i] = entries[i]
+            hs[place + 1 + i] = entries[i]
         return scale, entries
 
     def to_mixed(part, value):
         mixed[part, :] = value
 
-    def first():
-        loads["rhs"].wait()
-        loads["q0"].wait()
-        basis[0] = mixed[...]
-        leaf_terms(0, mixed[...])
-        pl.semaphore_wait(barrier, len(peers))
-        a = send_leaf(0)
-        pad_tree(0)
-        loads["e0"].wait()
-        block_product(0)
-        arrived(a)
-        low = tree(0, lambda: a_slot[0], False, while_z=begin_joins)
-        d = send_down(0, low)
-        left_device(a)
-        pad_tree(1)
-        arrived(d)
-
-        def to_image(part, value):
-            images[0, part, :] = value
-
-        spread_down(0, to_image)
-        left_device(d)
-        leaf_terms(1, images[0])
-        a = send_leaf(1)
-        loads["e1"].wait()
-        block_product(1)
-        arrived(a)
-        carried[0] = a_slot[1]
-        low = tree(1, lambda: carried[0], False, while_z=pass_joins)
-        d = send_down(1, low)
-        left_device(a)
-        arrived(d)
-        spread_down(1, to_mixed)
-        left_device(d)
-
     def iteration(j, carry):
-        before = j - 1
-        leaf_terms(0, mixed[...], partial_sums(before))
+        before = jnp.maximum(j - 1, 0)
+
+        def at_first(*steps):
+            @pl.when(j == 0)
+            def _():
+                for step in steps:
+                    step()
+
+        @pl.when(j > 0)
+        def _():
+            sums_ref[...] = partial_sums(before)
+
+        leaf_terms(0, mixed[...], sums_ref[...])
+        at_first(lambda: pl.semaphore_wait(barrier, len(peers)))
         a0 = send_leaf(0)
+        at_first(begin_joins, lambda: pad_tree(0), loads["e0"].wait)
         block_product(0)
         leaf_terms(1, direct[...])
         a1 = send_leaf(1)
         arrived(a0)
 
-        def weights_ready():
-            @pl.when(j == 1)
-            def _():
-                end_joins()
-
-        low = tree(0, lambda: a_slot[0], True, while_z=weights_ready)
+        low = tree(
+            0, lambda: a_slot[0], True,
+            while_z=lambda: at_first(lambda: pad_tree(1), lambda: turn_rows(0)),
+            while_x=lambda: at_first(pass_joins),
+        )
         d = send_down(0, low + riding(x_slot[0])[None])
+        at_first(end_joins)
 
         arrived(a1)
         sums = jnp.sum(x_slot[0, :, :, COLS:], axis=0)
         norm, scale, entries = column_entries(
-            lambda i: sums[:, RANK - COLS + i : RANK - COLS + i + 1], before
-        )
+            lambda i: sums[:, RANK - COLS + i : RANK - COLS + i + 1], j - 1
+        )
+        scale = jnp.where(j == 0, jnp.ones_like(scale), scale)
         carried[before] = carried[before] * scale[None]
         for i in range(GROUP):
             value = (a_slot[1, i] + joined_rows(low[i], i)) * scale
@@ -584,7 +564,8 @@
         def orthogonalise():
             arrived(d)
             totals = d_slot[0].reshape(COLS, LANES)[:, COLS:].T[RANK - COLS : RANK - COLS + 8]
-            scale, entries = arnoldi_column(totals, before)
+            scale, entries = arnoldi_column(totals, j - 1)
+            scale = jnp.where(j == 0, jnp.ones_like(scale), scale)
             basis[before] = basis[before] * scale
             images[before] = images[before] * scale
 
@@ -602,8 +583,13 @@
 
             spread_down(0, finish)
 
-        low = tree(1, lambda: fresh[...], False, while_x=orthogonalise)
+        low = tree(
+            1, lambda: fresh[...], False,
+            while_z=lambda: at_first(loads["p1"].wait, lambda: turn_rows(1)),
+            while_x=orthogonalise,
+        )
         e = send_down(1, low)
+        at_first(loads["e1"].wait)
         block_product(1)
         left_device(d)
         arrived(e)
@@ -611,8 +597,9 @@
         left_device(e)
         return carry
 
-    first()
-    lax.fori_loop(1, ITERS, iteration, 0)
+    loads["rhs"].wait()
+    loads["q0"].wait()
+    lax.fori_loop(0, ITERS, iteration, 0)
 
     totals = total_of(0, partial_sums(ITERS - 1))
     scale, entries = arnoldi_column(totals, ITERS - 1)
@@ -676,6 +663,7 @@
         pltpu.VMEM((2, DEEP, 8, COLS), F32),
         pltpu.VMEM((2, OUTER, 8, COLS), F32),
         pltpu.VMEM((ITERS * (ITERS + 1), 1, COLS), F32),
+        pltpu.VMEM((8, COLS), F32),
         pltpu.VMEM((GROUP, RANK, LANES), F32),
         pltpu.VMEM((GROUP, 2, LANES, LANES), BF16),
         pltpu.VMEM((ITERS,) + tree[1:], F32),

time: 148 us -> 134 us (0.905)
  Pallas kernels: 144 us -> 130 us
    pallas_call x1, Pallas kernels: 144 us -> 130 us  [on_device(): pl.pallas_call(kernel, out_shape=(jax.ShapeDtypeStruct((WIDTH, COLS), F32...]
where the time goes in v4:
time: 134 us; the launch traced here: 133 us
  Pallas kernels  130 us (97%)
  local copies, waits for them, and re-layouts  3.16 us (2%)
    pallas_call x1, Pallas kernels, on_device(): pl.pallas_call(kernel, out_shape=(jax.ShapeDtypeStruct((WIDTH, COLS), F32...  130 us

profile of v4, /device:TPU:1, one launch (start us, length us, event | category | flops | bytes accessed | tf_op | source)
XLA Modules:
  0.0 133.3 jit_solution(2738437007767746026)
XLA Ops:
  0.6 129.5 %shard_map.122 = (f32[1024,128]{1,0:T(8,128)}, f32[4,3,128]{2,1,0:T(4,128)}) custom-call(f32[1024,128]{1,0:T(8,128)} %rhs_hbm.1, bf16[1,1024,1024]{2,1,0:T(8,128)(2,1)} %ea_hbm.1, bf16[1,200,1024]{2,1,0:T(8,128)(2,1)} %pa_hbm.1, bf16[1,200,1024]{2,1,0:T(8,128)(2,1)} %qa_hbm.1, bf16[8,2,200,200]{3,2,1,0:T(8,128)(2,1)} %ta_hbm.1, ...), custom_call_target="tpu_custom_call" | custom-call | tf_op jit(solution)/shard_map/pallas_call | solution.py:691
  130.2 1.3 copy.13
  131.5 1.9 %copy.15 = f32[1024,128]{1,0:T(8,128)} copy(f32[1024,128]{1,0:T(8,128)} %get-tuple-element.6) | data formatting | bytes 1048576

commit v5 on v4

--- a/solution.py
+++ b/solution.py
@@ -21,6 +21,7 @@
 SLICE = COLS // GROUP
 LEVELS = 8
 TILE = 256
+SUMS = 16
 
 NT = (((1,), (1,)), ((), ()))
 NN = (((1,), (0,)), ((), ()))
@@ -46,6 +47,31 @@
     left = split[:, 0].reshape(count * SLICE, LANES)
     right = split[:, 1].reshape(count * SLICE, LANES)
     return left, right
+
+
+def two_sum(a, b):
+    total = a + b
+    shift = total - a
+    return total, (a - (total - shift)) + (b - shift)
+
+
+def add_exact(x, y):
+    high, low = two_sum(x[0], y[0])
+    low = low + (x[1] + y[1])
+    total = high + low
+    return total, low - (total - high)
+
+
+def times_exact(x, y):
+    a, b = x[0], y[0]
+    a_top = a.astype(BF16).astype(F32)
+    b_top = b.astype(BF16).astype(F32)
+    a_rest, b_rest = a - a_top, b - b_top
+    high = a * b
+    low = ((a_top * b_top - high) + a_top * b_rest + a_rest * b_top) + a_rest * b_rest
+    low = low + (a * y[1] + b * x[1])
+    total = high + low
+    return total, low - (total - high)
 
 
 def least_squares(entries, beta_first):
@@ -454,37 +480,30 @@
             high, join_w[i, 1], preferred_element_type=F32
         )
 
-    def total_of(which, rows):
-        r_send[which, 0] = rows
-        ra = copies(
-            GROUP, g, to_group, lambda k: r_send.at[which, 0],
-            ra_slot.at[which], ra_ss.at[which], ra_rs.at[which],
-        )
-        start(ra)
-        ra_slot[which, g] = rows
-        arrived(ra)
-        one = jnp.sum(ra_slot[which], axis=0)
-        r_send[which, 1] = one
-        rz = copies(
-            DEEP, zc, to_deep, lambda k: r_send.at[which, 1],
-            rz_slot.at[which], rz_ss.at[which], rz_rs.at[which],
-        )
-        start(rz)
-        rz_slot[which, zc] = one
-        arrived(rz)
-        two = jnp.sum(rz_slot[which], axis=0)
-        r_send[which, 2] = two
-        rx = copies(
-            OUTER, xc, to_outer, lambda k: r_send.at[which, 2],
-            rx_slot.at[which], rx_ss.at[which], rx_rs.at[which],
-        )
-        start(rx)
-        rx_slot[which, xc] = two
-        arrived(rx)
-        left_device(ra)
-        left_device(rz)
-        left_device(rx)
-        return jnp.sum(rx_slot[which], axis=0)
+    def total_of(high, low):
+        def gather(stage, rows, count, coord, target, slot, send_sem, recv_sem):
+            r_send[stage] = rows
+            group = copies(
+                count, coord, target, lambda k: r_send.at[stage], slot, send_sem, recv_sem
+            )
+            start(group)
+            slot[coord] = rows
+            arrived(group)
+            half = SUMS
+            pairs_in = [(slot[i, :half], slot[i, half:]) for i in range(count)]
+            while len(pairs_in) > 1:
+                pairs_in = [
+                    add_exact(pairs_in[i], pairs_in[i + 1]) for i in range(0, len(pairs_in), 2)
+                ]
+            return group, jnp.concatenate(pairs_in[0], axis=0)
+
+        rows = jnp.concatenate([high, low], axis=0)
+        ra, rows = gather(0, rows, GROUP, g, to_group, ra_slot, ra_ss, ra_rs)
+        rz, rows = gather(1, rows, DEEP, zc, to_deep, rz_slot, rz_ss, rz_rs)
+        rx, rows = gather(2, rows, OUTER, xc, to_outer, rx_slot, rx_ss, rx_rs)
+        for group in (ra, rz, rx):
+            left_device(group)
+        return rows
 
     def column_sum(x):
         return jnp.sum(x, axis=0, keepdims=True)
@@ -601,16 +620,57 @@
     loads["q0"].wait()
     lax.fori_loop(0, ITERS, iteration, 0)
 
-    totals = total_of(0, partial_sums(ITERS - 1))
-    scale, entries = arnoldi_column(totals, ITERS - 1)
-    basis[ITERS - 1] = basis[ITERS - 1] * scale
-    images[ITERS - 1] = images[ITERS - 1] * scale
-    update = mixed[...] * scale
+    earlier_norm = hs[(ITERS - 2) * (ITERS + 1)]
+    shrink = 1.0 / earlier_norm
+    which = [(0, 3), (1, 3), (2, 3), (2, 2), (3, 3), (0, 0), (0, 1), (0, 2), (1, 1), (1, 2)]
+    step = 64
+
+    def one_step(t, carry):
+        rows = pl.ds(pl.multiple_of(t * step, step), step)
+        parts = [basis[i, rows, :] for i in range(ITERS)] + [mixed[rows, :] * shrink]
+        out = []
+        for (first, second), total in zip(which, carry):
+            term = jnp.sum((parts[first] * parts[second]).reshape(step // 8, 8, COLS), axis=0)
+            high, low = two_sum(total[0], term)
+            out.append((high, total[1] + low))
+        return tuple(out)
+
+    nothing = jnp.zeros((8, COLS), F32)
+    sums = lax.fori_loop(0, WIDTH // step, one_step, ((nothing, nothing),) * len(which))
+    highs, lows = [], []
+    for total in sums:
+        for shift in (4, 2, 1):
+            total = add_exact(total, tuple(pltpu.roll(x, shift, 0) for x in total))
+        highs.append(total[0][0:1])
+        lows.append(total[1][0:1])
+    rest = [jnp.zeros((SUMS - len(which), COLS), F32)]
+    totals = total_of(
+        jnp.concatenate(highs + rest, axis=0), jnp.concatenate(lows + rest, axis=0)
+    )
+    inner = {
+        pair: (totals[i : i + 1], totals[SUMS + i : SUMS + i + 1]) for i, pair in enumerate(which)
+    }
+    norm = jnp.sqrt(inner[2, 2][0] + EPSILON)
+    hs[(ITERS - 1) * (ITERS + 1)] = norm
+    lead = earlier_norm / norm
+    weights_of = []
     for i in range(ITERS):
-        update = update - entries[i] * basis[i]
-    last = column_sum(update * update)
-    totals = total_of(1, jnp.concatenate([last, jnp.zeros((7, COLS), F32)], axis=0))
-    last_norm = jnp.sqrt(totals[0:1] + EPSILON)
+        entry = inner[i, ITERS][0] * lead
+        if i == ITERS - 1:
+            entry = entry / norm
+        hs[(ITERS - 1) * (ITERS + 1) + 1 + i] = entry
+        weights_of.append(-entry if i < ITERS - 1 else -(entry / norm))
+    weights_of.append(lead)
+    square = None
+    for first, second in which:
+        plain = (weights_of[first], jnp.zeros_like(norm))
+        other = (weights_of[second], jnp.zeros_like(norm))
+        term = times_exact(times_exact(plain, other), inner[first, second])
+        if first != second:
+            term = (2.0 * term[0], 2.0 * term[1])
+        square = term if square is None else add_exact(square, term)
+    last_norm = jnp.sqrt(jnp.maximum(square[0], jnp.zeros_like(norm)) + EPSILON)
+    scale = 1.0 / norm
     zero = jnp.zeros((1, COLS), F32)
     entries = [[zero for column in range(ITERS)] for line in range(ITERS + 1)]
     for column in range(ITERS):
@@ -621,6 +681,7 @@
         else:
             entries[column + 1][column] = last_norm
     weights = least_squares(entries, hs[0])
+    weights[ITERS - 1] = weights[ITERS - 1] * scale
     sol_ref[...] = weights[0] * images[0] + weights[1] * images[1] + weights[2] * images[2]
     for line in range(ITERS + 1):
         hess_ref[line] = jnp.concatenate(entries[line], axis=0)
@@ -658,10 +719,10 @@
         pltpu.VMEM((8, SLICE, LANES), F32),
         pltpu.VMEM((4, SLICE, LANES), F32),
         pltpu.VMEM((2, SLICE, LANES), F32),
-        pltpu.VMEM((2, 3, 8, COLS), F32),
-        pltpu.VMEM((2, GROUP, 8, COLS), F32),
-        pltpu.VMEM((2, DEEP, 8, COLS), F32),
-        pltpu.VMEM((2, OUTER, 8, COLS), F32),
+        pltpu.VMEM((3, 2 * SUMS, COLS), F32),
+        pltpu.VMEM((GROUP, 2 * SUMS, COLS), F32),
+        pltpu.VMEM((DEEP, 2 * SUMS, COLS), F32),
+        pltpu.VMEM((OUTER, 2 * SUMS, COLS), F32),
         pltpu.VMEM((ITERS * (ITERS + 1), 1, COLS), F32),
         pltpu.VMEM((8, COLS), F32),
         pltpu.VMEM((GROUP, RANK, LANES), F32),
@@ -677,12 +738,12 @@
         dma((2, OUTER - 1)),
         dma((2, GROUP - 1)),
         dma((2, GROUP - 1)),
-        dma((2, GROUP - 1)),
-        dma((2, GROUP - 1)),
-        dma((2, DEEP - 1)),
-        dma((2, DEEP - 1)),
-        dma((2, OUTER - 1)),
-        dma((2, OUTER - 1)),
+        dma((GROUP - 1,)),
+        dma((GROUP - 1,)),
+        dma((DEEP - 1,)),
+        dma((DEEP - 1,)),
+        dma((OUTER - 1,)),
+        dma((OUTER - 1,)),
         dma((7,)),
         dma((7,)),
     ]

time: 134 us -> 123 us (0.918)
  Pallas kernels: 130 us -> 119 us
    pallas_call x1, Pallas kernels: 130 us -> 119 us  [on_device(): pl.pallas_call(kernel, out_shape=(jax.ShapeDtypeStruct((WIDTH, COLS), F32...]
where the time goes in v5:
time: 123 us
  Pallas kernels  119 us (97%)
  local copies, waits for them, and re-layouts  3.16 us (3%)
    pallas_call x1, Pallas kernels, on_device(): pl.pallas_call(kernel, out_shape=(jax.ShapeDtypeStruct((WIDTH, COLS), F32...  119 us

profile of v5, /device:TPU:1, one launch (start us, length us, event | category | flops | bytes accessed | tf_op | source)
XLA Modules:
  0.0 123.2 jit_solution(15906450677447849066)
XLA Ops:
  0.6 119.4 %shard_map.122 = (f32[1024,128]{1,0:T(8,128)}, f32[4,3,128]{2,1,0:T(4,128)}) custom-call(f32[1024,128]{1,0:T(8,128)} %rhs_hbm.1, bf16[1,1024,1024]{2,1,0:T(8,128)(2,1)} %ea_hbm.1, bf16[1,200,1024]{2,1,0:T(8,128)(2,1)} %pa_hbm.1, bf16[1,200,1024]{2,1,0:T(8,128)(2,1)} %qa_hbm.1, bf16[8,2,200,200]{3,2,1,0:T(8,128)(2,1)} %ta_hbm.1, ...), custom_call_target="tpu_custom_call" | custom-call | tf_op jit(solution)/shard_map/pallas_call | solution.py:752
  120.0 1.3 %copy.13 = f32[4,3,128]{2,0,1:T(4,128)} copy(f32[4,3,128]{2,1,0:T(4,128)} %get-tuple-element.3) | data formatting | bytes 12288 | tf_op jit(solution)/shard_map/pallas_call | solution.py:752
  121.3 1.9 %copy.15 = f32[1024,128]{1,0:T(8,128)} copy(f32[1024,128]{1,0:T(8,128)} %get-tuple-element.6) | data formatting | bytes 1048576

commit v6 on v5

--- a/solution.py
+++ b/solution.py
@@ -153,7 +153,9 @@
     joins,
     join_w,
     carried,
-    fresh,
+    fresh_m,
+    fresh_a,
+    applied,
     load_sem,
     a_ss,
     a_rs,
@@ -194,13 +196,13 @@
         "q0": load(qm_hbm.at[0], cols_side.at[0], 1),
         "p0": load(pm_hbm.at[0], rows_raw.at[0], 5),
         "q1": load(qa_hbm.at[0], cols_side.at[1], 6),
+        "p1": load(pa_hbm.at[0], rows_raw.at[1], 10),
         "t0": load(tm_hbm, trans_raw.at[0], 2),
         "e0": load(em_hbm.at[0], blocks.at[0], 3),
         "c0": load(cm_hbm, coup_raw.at[0], 4),
         "t1": load(ta_hbm, trans_raw.at[1], 7),
         "e1": load(ea_hbm.at[0], blocks.at[1], 8),
         "c1": load(ca_hbm, coup_raw.at[1], 9),
-        "p1": load(pa_hbm.at[0], rows_raw.at[1], 10),
     }
     for item in loads.values():
         item.start()
@@ -217,6 +219,8 @@
         basis[i] = jnp.zeros((WIDTH, COLS), F32)
         images[i] = jnp.zeros((WIDTH, COLS), F32)
         carried[i] = jnp.zeros((GROUP, SLICE, LANES), F32)
+    for i in range(ITERS - 1):
+        applied[i] = jnp.zeros((WIDTH, COLS), F32)
 
     def pad_tree(op):
         loads["t%d" % op].wait()
@@ -312,10 +316,12 @@
         total = jnp.where(lane >= RANK - COLS, total, jnp.zeros_like(total))
         return jnp.concatenate([jnp.zeros((SLICE, COLS), F32), total], axis=1)
 
-    def leaf_terms(op, value, sums=None):
+    def leaf_terms(op, value, sums=None, only_stack=False):
         high, low = halves(value)
         stacked[:, :COLS] = high
         stacked[:, COLS:] = low
+        if only_stack:
+            return
         both = jnp.dot(cols_side[op], stacked[...], preferred_element_type=F32)
         leaf = both[:, :COLS] + both[:, COLS:]
         rest = LANES - RANK
@@ -326,24 +332,30 @@
             leaf = jnp.concatenate([leaf, sums, pad], axis=0)
         a_send[op] = leaf.T.reshape(GROUP, SLICE, LANES)
 
-    def send_leaf(op):
-        a = copies(
+    def leaf_copies(op):
+        return copies(
             GROUP, g, to_group, lambda k: a_send.at[op, (g + k) % GROUP],
             a_slot.at[op], a_ss.at[op], a_rs.at[op],
         )
-        start(a)
+
+    def down_copies(op):
+        return copies(
+            GROUP, g, to_group, lambda k: d_send.at[op, (g + k) % GROUP],
+            d_slot.at[op], d_ss.at[op], d_rs.at[op],
+        )
+
+    def send_leaf(op):
+        start(leaf_copies(op))
         a_slot[op, g] = a_send[op, g]
-        return a
 
     def send_down(op, value):
         d_send[op] = value
-        d = copies(
-            GROUP, g, to_group, lambda k: d_send.at[op, (g + k) % GROUP],
-            d_slot.at[op], d_ss.at[op], d_rs.at[op],
-        )
-        start(d)
+        start(down_copies(op))
         d_slot[op, g] = d_send[op, g]
-        return d
+
+    def finished(group):
+        arrived(group)
+        left_device(group)
 
     def block_product(op):
         for t in range(WIDTH // TILE):
@@ -416,68 +428,65 @@
         return d0
 
     partner = g + 1 - 2 * (g % 2)
-    join_out = []
-    join_in = []
-    for k in range(4):
-        to = to_group(2 * k) if k else (me // GROUP) * GROUP + partner
-        source = (g + GROUP - 2 * k) % GROUP if k else partner
-        for group, where in ((join_out, g), (join_in, source)):
-            group.append(
-                pltpu.make_async_remote_copy(
-                    src_ref=joins.at[g], dst_ref=joins.at[where],
-                    send_sem=j_ss.at[k], recv_sem=j_rs.at[k],
-                    device_id=(to,), device_id_type=MESH,
-                )
-            )
-    pass_out = []
-    pass_in = []
-    for k in range(1, 4):
-        mine = (g + GROUP - 2 * k) % GROUP
-        theirs = (partner + GROUP - 2 * k) % GROUP
-        for group, where in ((pass_out, mine), (pass_in, theirs)):
-            group.append(
-                pltpu.make_async_remote_copy(
-                    src_ref=joins.at[mine], dst_ref=joins.at[where],
-                    send_sem=j_ss.at[3 + k], recv_sem=j_rs.at[3 + k],
-                    device_id=((me // GROUP) * GROUP + partner,), device_id_type=MESH,
-                )
-            )
-
-    def begin_joins():
-        loads["p0"].wait()
-        loads["q1"].wait()
-        own = lax.dot_general(rows_raw[0], cols_side[1], NT, preferred_element_type=F32)
-        joins[g] = jnp.pad(own, ((0, 0), (0, LANES - RANK)))
-        for c in join_out:
+    to_partner = (me // GROUP) * GROUP + partner
+
+    def join_copy(op, source, where, k, to):
+        return pltpu.make_async_remote_copy(
+            src_ref=joins.at[op, source], dst_ref=joins.at[op, where],
+            send_sem=j_ss.at[op, k], recv_sem=j_rs.at[op, k],
+            device_id=(to,), device_id_type=MESH,
+        )
+
+    def join_copies(op):
+        out = [join_copy(op, g, g, 0, to_partner)]
+        into = [join_copy(op, g, partner, 0, to_partner)]
+        for k in range(1, 4):
+            out.append(join_copy(op, g, g, k, to_group(2 * k)))
+            into.append(join_copy(op, g, (g + GROUP - 2 * k) % GROUP, k, to_group(2 * k)))
+        return out, into
+
+    def pass_copies(op):
+        out, into = [], []
+        for k in range(1, 4):
+            mine = (g + GROUP - 2 * k) % GROUP
+            theirs = (partner + GROUP - 2 * k) % GROUP
+            out.append(join_copy(op, mine, mine, 3 + k, to_partner))
+            into.append(join_copy(op, mine, theirs, 3 + k, to_partner))
+        return out, into
+
+    def begin_joins(op):
+        own = lax.dot_general(rows_raw[op], cols_side[1 - op], NT, preferred_element_type=F32)
+        joins[op, g] = jnp.pad(own, ((0, 0), (0, LANES - RANK)))
+        for c in join_copies(op)[0]:
             c.start()
 
-    def pass_joins():
-        for k in range(1, 4):
-            join_in[k].wait_recv()
-            pass_out[k - 1].start()
-
-    def end_joins():
-        join_in[0].wait_recv()
-        for c in pass_in:
+    def pass_joins(op):
+        for came, further in zip(join_copies(op)[1][1:], pass_copies(op)[0]):
+            came.wait_recv()
+            further.start()
+
+    def end_joins(op):
+        join_copies(op)[1][0].wait_recv()
+        for c in pass_copies(op)[1]:
             c.wait_recv()
 
         def one(i, carry):
-            high, low = halves(jnp.pad(joins[i], ((0, LANES - RANK), (0, 0))))
-            join_w[i, 0] = high
-            join_w[i, 1] = low
+            high, low = halves(jnp.pad(joins[op, i], ((0, LANES - RANK), (0, 0))))
+            join_w[op, i, 0] = high
+            join_w[op, i, 1] = low
             return carry
 
         lax.fori_loop(0, GROUP, one, 0)
-        for c in join_out + pass_out:
+        for c in join_copies(op)[0] + pass_copies(op)[0]:
             c.wait_send()
 
-    def joined_rows(x, i):
+    def joined_rows(op, x, i):
         high, low = halves(x)
         main = jnp.dot(
-            jnp.concatenate([high, low], axis=0), join_w[i, 0], preferred_element_type=F32
+            jnp.concatenate([high, low], axis=0), join_w[op, i, 0], preferred_element_type=F32
         )
         return main[:SLICE] + main[SLICE:] + jnp.dot(
-            high, join_w[i, 1], preferred_element_type=F32
+            high, join_w[op, i, 1], preferred_element_type=F32
         )
 
     def total_of(high, low):
@@ -531,8 +540,30 @@
             hs[place + 1 + i] = entries[i]
         return scale, entries
 
-    def to_mixed(part, value):
-        mixed[part, :] = value
+    def settle(j):
+        d = down_copies(1)
+        finished(d)
+        totals = d_slot[1].reshape(COLS, LANES)[:, COLS:].T[RANK - COLS : RANK - COLS + 8]
+        scale, entries = arnoldi_column(totals, j - 1)
+        scale = jnp.where(j == 0, jnp.ones_like(scale), scale)
+        before = jnp.maximum(j - 1, 0)
+        basis[before] = basis[before] * scale
+        images[before] = images[before] * scale
+        applied[before] = mixed[...] * scale
+
+        def finish(part, value):
+            value = value * scale
+            update = mixed[part, :] * scale
+            image = images[j, part, :] * scale
+            for i in range(ITERS - 1):
+                value = value - entries[i] * applied[i, part, :]
+                update = update - entries[i] * basis[i, part, :]
+                image = image - entries[i] * images[i, part, :]
+            basis[j, part, :] = update
+            images[j, part, :] = image
+            mixed[part, :] = value
+
+        spread_down(1, finish)
 
     def iteration(j, carry):
         before = jnp.maximum(j - 1, 0)
@@ -543,82 +574,92 @@
                 for step in steps:
                     step()
 
-        @pl.when(j > 0)
-        def _():
-            sums_ref[...] = partial_sums(before)
-
-        leaf_terms(0, mixed[...], sums_ref[...])
-        at_first(lambda: pl.semaphore_wait(barrier, len(peers)))
-        a0 = send_leaf(0)
-        at_first(begin_joins, lambda: pad_tree(0), loads["e0"].wait)
-        block_product(0)
-        leaf_terms(1, direct[...])
-        a1 = send_leaf(1)
-        arrived(a0)
+        def in_m_tree():
+            at_first(lambda: pad_tree(1), lambda: turn_rows(0))
+
+            @pl.when(j > 0)
+            def _():
+                settle(before)
+                sums_ref[...] = partial_sums(before)
+                leaf_terms(0, mixed[...], only_stack=True)
+                block_product(0)
+                leaf_terms(1, direct[...], sums_ref[...])
+                send_leaf(1)
 
         low = tree(
-            0, lambda: a_slot[0], True,
-            while_z=lambda: at_first(lambda: pad_tree(1), lambda: turn_rows(0)),
-            while_x=lambda: at_first(pass_joins),
-        )
-        d = send_down(0, low + riding(x_slot[0])[None])
-        at_first(end_joins)
-
-        arrived(a1)
-        sums = jnp.sum(x_slot[0, :, :, COLS:], axis=0)
-        norm, scale, entries = column_entries(
-            lambda i: sums[:, RANK - COLS + i : RANK - COLS + i + 1], j - 1
-        )
-        scale = jnp.where(j == 0, jnp.ones_like(scale), scale)
-        carried[before] = carried[before] * scale[None]
+            0, lambda: fresh_m[...], False,
+            while_z=in_m_tree, while_x=lambda: at_first(lambda: pass_joins(0)),
+        )
+        send_down(0, low)
+        at_first(lambda: end_joins(0))
+        finished(leaf_copies(1))
         for i in range(GROUP):
-            value = (a_slot[1, i] + joined_rows(low[i], i)) * scale
-            for earlier in range(ITERS - 1):
-                value = value - entries[earlier] * carried[earlier, i]
-            fresh[i] = value
-        carried[j] = fresh[...]
-        left_device(a0)
-        left_device(a1)
-
-        def orthogonalise():
-            arrived(d)
-            totals = d_slot[0].reshape(COLS, LANES)[:, COLS:].T[RANK - COLS : RANK - COLS + 8]
-            scale, entries = arnoldi_column(totals, j - 1)
-            scale = jnp.where(j == 0, jnp.ones_like(scale), scale)
-            basis[before] = basis[before] * scale
-            images[before] = images[before] * scale
-
-            def finish(part, image):
-                image = image * scale
-                update = mixed[part, :] * scale
-                for i in range(ITERS - 1):
-                    image = image - entries[i] * images[i, part, :]
-                    update = update - entries[i] * basis[i, part, :]
-                images[j, part, :] = image
-                basis[j, part, :] = update
-                high, low = halves(image)
+            fresh_a[i] = a_slot[1, i] + joined_rows(0, low[i], i)
+
+        def in_a_tree():
+            at_first(lambda: turn_rows(1))
+            d = down_copies(0)
+            finished(d)
+
+            def to_image(part, value):
+                images[j, part, :] = value
+                high, low = halves(value)
                 stacked[part, :COLS] = high
                 stacked[part, COLS:] = low
 
-            spread_down(0, finish)
+            spread_down(0, to_image)
+            at_first(loads["e1"].wait)
+            block_product(1)
+
+            @pl.when(j < ITERS - 1)
+            def _():
+                leaf_terms(0, direct[...])
+                send_leaf(0)
 
         low = tree(
-            1, lambda: fresh[...], False,
-            while_z=lambda: at_first(loads["p1"].wait, lambda: turn_rows(1)),
-            while_x=orthogonalise,
-        )
-        e = send_down(1, low)
-        at_first(loads["e1"].wait)
-        block_product(1)
-        left_device(d)
-        arrived(e)
-        spread_down(1, to_mixed)
-        left_device(e)
+            1, lambda: fresh_a[...], True,
+            while_z=in_a_tree, while_x=lambda: at_first(lambda: pass_joins(1)),
+        )
+        send_down(1, low + riding(x_slot[1])[None])
+        at_first(lambda: end_joins(1))
+
+        @pl.when(j < ITERS - 1)
+        def _():
+            finished(leaf_copies(0))
+            sums = jnp.sum(x_slot[1, :, :, COLS:], axis=0)
+            norm, scale, entries = column_entries(
+                lambda i: sums[:, RANK - COLS + i : RANK - COLS + i + 1], j - 1
+            )
+            scale = jnp.where(j == 0, jnp.ones_like(scale), scale)
+            carried[before] = carried[before] * scale[None]
+            for i in range(GROUP):
+                value = (a_slot[0, i] + joined_rows(1, low[i], i)) * scale
+                for earlier in range(ITERS - 2):
+                    value = value - entries[earlier] * carried[earlier, i]
+                fresh_m[i] = value
+            carried[j] = fresh_m[...]
+
         return carry
 
     loads["rhs"].wait()
     loads["q0"].wait()
+    leaf_terms(0, mixed[...])
+    pl.semaphore_wait(barrier, len(peers))
+    send_leaf(0)
+    loads["p0"].wait()
+    loads["q1"].wait()
+    begin_joins(0)
+    pad_tree(0)
+    loads["e0"].wait()
+    block_product(0)
+    leaf_terms(1, direct[...], sums_ref[...])
+    send_leaf(1)
+    loads["p1"].wait()
+    begin_joins(1)
+    finished(leaf_copies(0))
+    fresh_m[...] = a_slot[0]
     lax.fori_loop(0, ITERS, iteration, 0)
+    settle(ITERS - 1)
 
     earlier_norm = hs[(ITERS - 2) * (ITERS + 1)]
     shrink = 1.0 / earlier_norm
@@ -725,10 +766,12 @@
         pltpu.VMEM((OUTER, 2 * SUMS, COLS), F32),
         pltpu.VMEM((ITERS * (ITERS + 1), 1, COLS), F32),
         pltpu.VMEM((8, COLS), F32),
-        pltpu.VMEM((GROUP, RANK, LANES), F32),
-        pltpu.VMEM((GROUP, 2, LANES, LANES), BF16),
+        pltpu.VMEM((2, GROUP, RANK, LANES), F32),
+        pltpu.VMEM((2, GROUP, 2, LANES, LANES), BF16),
         pltpu.VMEM((ITERS,) + tree[1:], F32),
         pltpu.VMEM(tree[1:], F32),
+        pltpu.VMEM(tree[1:], F32),
+        pltpu.VMEM((ITERS - 1, WIDTH, COLS), F32),
         dma((11,)),
         dma((2, GROUP - 1)),
         dma((2, GROUP - 1)),
@@ -744,8 +787,8 @@
         dma((DEEP - 1,)),
         dma((OUTER - 1,)),
         dma((OUTER - 1,)),
-        dma((7,)),
-        dma((7,)),
+        dma((2, 7)),
+        dma((2, 7)),
     ]
 
     def on_device(*args):

time: 123 us -> 109 us (0.89)
  Pallas kernels: 119 us -> 104 us
    pallas_call x1, Pallas kernels: 119 us -> 104 us  [on_device(): pl.pallas_call(kernel, out_shape=(jax.ShapeDtypeStruct((WIDTH, COLS), F32...]
where the time goes in v6:
time: 109 us; the launch traced here: 108 us
  Pallas kernels  104 us (95%)
  local copies, waits for them, and re-layouts  3.16 us (3%)
    pallas_call x1, Pallas kernels, on_device(): pl.pallas_call(kernel, out_shape=(jax.ShapeDtypeStruct((WIDTH, COLS), F32...  104 us

profile of v6, /device:TPU:1, one launch (start us, length us, event | category | flops | bytes accessed | tf_op | source)
XLA Modules:
  0.0 108.1 jit_solution(16673913008169467375)
XLA Ops:
  0.6 104.3 %shard_map.122 = (f32[1024,128]{1,0:T(8,128)}, f32[4,3,128]{2,1,0:T(4,128)}) custom-call(f32[1024,128]{1,0:T(8,128)} %rhs_hbm.1, bf16[1,1024,1024]{2,1,0:T(8,128)(2,1)} %ea_hbm.1, bf16[1,200,1024]{2,1,0:T(8,128)(2,1)} %pa_hbm.1, bf16[1,200,1024]{2,1,0:T(8,128)(2,1)} %qa_hbm.1, bf16[8,2,200,200]{3,2,1,0:T(8,128)(2,1)} %ta_hbm.1, ...), custom_call_target="tpu_custom_call" | custom-call | tf_op jit(solution)/shard_map/pallas_call | solution.py:795
  104.9 1.3 %copy.13 = f32[4,3,128]{2,0,1:T(4,128)} copy(f32[4,3,128]{2,1,0:T(4,128)} %get-tuple-element.3) | data formatting | bytes 12288 | tf_op jit(solution)/shard_map/pallas_call | solution.py:795
  106.2 1.9 %copy.15 = f32[1024,128]{1,0:T(8,128)} copy(f32[1024,128]{1,0:T(8,128)} %get-tuple-element.6) | data formatting | bytes 1048576

commit v7 on v6

--- a/solution.py
+++ b/solution.py
@@ -21,7 +21,7 @@
 SLICE = COLS // GROUP
 LEVELS = 8
 TILE = 256
-SUMS = 16
+SUMS = 12
 
 NT = (((1,), (1,)), ((), ()))
 NN = (((1,), (0,)), ((), ()))
@@ -222,9 +222,10 @@
     for i in range(ITERS - 1):
         applied[i] = jnp.zeros((WIDTH, COLS), F32)
 
-    def pad_tree(op):
-        loads["t%d" % op].wait()
-        loads["c%d" % op].wait()
+    def pad_tree(op, low, high):
+        if low == 0:
+            loads["t%d" % op].wait()
+            loads["c%d" % op].wait()
         edge = ((0, LANES - RANK), (0, LANES - RANK))
 
         def one(h, carry):
@@ -233,7 +234,7 @@
                 coup[op, h, s] = jnp.pad(coup_raw[op, h, s], edge)
             return carry
 
-        lax.fori_loop(0, LEVELS, one, 0)
+        lax.fori_loop(low, high, one, 0)
 
     def turn_rows(op):
         for t in range(WIDTH // TILE):
@@ -489,7 +490,7 @@
             high, join_w[op, i, 1], preferred_element_type=F32
         )
 
-    def total_of(high, low):
+    def total_of(high, low, meanwhile):
         def gather(stage, rows, count, coord, target, slot, send_sem, recv_sem):
             r_send[stage] = rows
             group = copies(
@@ -497,6 +498,8 @@
             )
             start(group)
             slot[coord] = rows
+            if stage == 0:
+                meanwhile()
             arrived(group)
             half = SUMS
             pairs_in = [(slot[i, :half], slot[i, half:]) for i in range(count)]
@@ -540,7 +543,7 @@
             hs[place + 1 + i] = entries[i]
         return scale, entries
 
-    def settle(j):
+    def settle(j, last=False):
         d = down_copies(1)
         finished(d)
         totals = d_slot[1].reshape(COLS, LANES)[:, COLS:].T[RANK - COLS : RANK - COLS + 8]
@@ -548,22 +551,33 @@
         scale = jnp.where(j == 0, jnp.ones_like(scale), scale)
         before = jnp.maximum(j - 1, 0)
         basis[before] = basis[before] * scale
-        images[before] = images[before] * scale
-        applied[before] = mixed[...] * scale
+        if not last:
+            applied[before] = mixed[...] * scale
 
         def finish(part, value):
             value = value * scale
             update = mixed[part, :] * scale
-            image = images[j, part, :] * scale
             for i in range(ITERS - 1):
-                value = value - entries[i] * applied[i, part, :]
+                held = update if last and i == ITERS - 2 else applied[i, part, :]
+                value = value - entries[i] * held
+            for i in range(ITERS - 1):
                 update = update - entries[i] * basis[i, part, :]
-                image = image - entries[i] * images[i, part, :]
             basis[j, part, :] = update
-            images[j, part, :] = image
             mixed[part, :] = value
+            if not last:
+                high, low = halves(value)
+                stacked[part, :COLS] = high
+                stacked[part, COLS:] = low
+
+        def finish_images():
+            images[before] = images[before] * scale
+            image = images[j] * scale
+            for i in range(ITERS - 1):
+                image = image - entries[i] * images[i]
+            images[j] = image
 
         spread_down(1, finish)
+        return finish_images
 
     def iteration(j, carry):
         before = jnp.maximum(j - 1, 0)
@@ -575,16 +589,18 @@
                     step()
 
         def in_m_tree():
-            at_first(lambda: pad_tree(1), lambda: turn_rows(0))
+            at_first(
+                lambda: pad_tree(0, 3, LEVELS), lambda: pad_tree(1, 0, LEVELS), lambda: turn_rows(0)
+            )
 
             @pl.when(j > 0)
             def _():
-                settle(before)
+                finish_images = settle(before)
                 sums_ref[...] = partial_sums(before)
-                leaf_terms(0, mixed[...], only_stack=True)
                 block_product(0)
                 leaf_terms(1, direct[...], sums_ref[...])
                 send_leaf(1)
+                finish_images()
 
         low = tree(
             0, lambda: fresh_m[...], False,
@@ -649,7 +665,7 @@
     loads["p0"].wait()
     loads["q1"].wait()
     begin_joins(0)
-    pad_tree(0)
+    pad_tree(0, 0, 3)
     loads["e0"].wait()
     block_product(0)
     leaf_terms(1, direct[...], sums_ref[...])
@@ -659,7 +675,7 @@
     finished(leaf_copies(0))
     fresh_m[...] = a_slot[0]
     lax.fori_loop(0, ITERS, iteration, 0)
-    settle(ITERS - 1)
+    finish_images = settle(ITERS - 1, last=True)
 
     earlier_norm = hs[(ITERS - 2) * (ITERS + 1)]
     shrink = 1.0 / earlier_norm
@@ -686,7 +702,9 @@
         lows.append(total[1][0:1])
     rest = [jnp.zeros((SUMS - len(which), COLS), F32)]
     totals = total_of(
-        jnp.concatenate(highs + rest, axis=0), jnp.concatenate(lows + rest, axis=0)
+        jnp.concatenate(highs + rest, axis=0),
+        jnp.concatenate(lows + rest, axis=0),
+        finish_images,
     )
     inner = {
         pair: (totals[i : i + 1], totals[SUMS + i : SUMS + i + 1]) for i, pair in enumerate(which)
@@ -725,7 +743,8 @@
     weights[ITERS - 1] = weights[ITERS - 1] * scale
     sol_ref[...] = weights[0] * images[0] + weights[1] * images[1] + weights[2] * images[2]
     for line in range(ITERS + 1):
-        hess_ref[line] = jnp.concatenate(entries[line], axis=0)
+        for column in range(ITERS):
+            hess_ref[column, line : line + 1, :] = entries[line][column]
 
 
 def solution(mesh):
@@ -791,12 +810,16 @@
         dma((2, 7)),
     ]
 
+    def hand_over(sol_in, hess_in, sol_out, hess_out):
+        sol_out[...] = sol_in[...]
+        hess_out[...] = hess_in[...]
+
     def on_device(*args):
-        return pl.pallas_call(
+        both = pl.pallas_call(
             kernel,
             out_shape=(
                 jax.ShapeDtypeStruct((WIDTH, COLS), F32),
-                jax.ShapeDtypeStruct((ITERS + 1, ITERS, COLS), F32),
+                jax.ShapeDtypeStruct((ITERS, ITERS + 1, COLS), F32),
             ),
             in_specs=[pl.BlockSpec(memory_space=pl.ANY)] * 11,
             out_specs=[pl.BlockSpec(memory_space=pltpu.VMEM)] * 2,
@@ -805,6 +828,13 @@
                 collective_id=0, has_side_effects=True, vmem_limit_bytes=60 * 2**20
             ),
         )(*args)
+        sol, hess = pl.pallas_call(
+            hand_over,
+            out_shape=tuple(jax.ShapeDtypeStruct(x.shape, x.dtype) for x in both),
+            in_specs=[pl.BlockSpec(memory_space=pltpu.VMEM)] * 2,
+            out_specs=[pl.BlockSpec(memory_space=pltpu.VMEM)] * 2,
+        )(*both)
+        return sol, jnp.swapaxes(hess, 0, 1)
 
     leaf = P("leaf", None)
     block = P("leaf", None, None)

time: 109 us -> 106 us (0.972); the launches traced: 108 us -> 106 us
  local copies, waits for them, and re-layouts: 3.16 us -> 0 us
  Pallas kernels: 104 us -> 106 us
    pallas_call x0 -> x1, Pallas kernels: none -> 1.87 us  [on_device(): pl.pallas_call(hand_over, out_shape=tuple((jax.ShapeDtypeStruct(x.shape,...]
    unnamed x1 -> x0, local copies, waits for them, and re-layouts: 1.87 us -> none
    pallas_call x1 -> x0, local copies, waits for them, and re-layouts: 1.29 us -> none  [on_device(): pl.pallas_call(kernel, out_shape=(jax.ShapeDtypeStruct((WIDTH, COLS), F32...]
where the time goes in v7:
time: 106 us
  Pallas kernels  106 us (100%)
    pallas_call x1, Pallas kernels, on_device(): pl.pallas_call(kernel, out_shape=(jax.ShapeDtypeStruct((WIDTH, COLS), F32...  104 us

profile of v7, /device:TPU:1, one launch (start us, length us, event | category | flops | bytes accessed | tf_op | source)
XLA Modules:
  0.0 106.3 jit_solution(16071210168056970064)
XLA Ops:
  0.6 103.8 %shard_map.122 = (f32[1024,128]{1,0:T(8,128)}, f32[3,4,128]{2,1,0:T(4,128)}) custom-call(f32[1024,128]{1,0:T(8,128)} %rhs_hbm.1, bf16[1,1024,1024]{2,1,0:T(8,128)(2,1)} %ea_hbm.1, bf16[1,200,1024]{2,1,0:T(8,128)(2,1)} %pa_hbm.1, bf16[1,200,1024]{2,1,0:T(8,128)(2,1)} %qa_hbm.1, bf16[8,2,200,200]{3,2,1,0:T(8,128)(2,1)} %ta_hbm.1, ...), custom_call_target="tpu_custom_call" | custom-call | tf_op jit(solution)/shard_map/pallas_call | solution.py:818
  104.4 1.9 %shard_map.123 = (f32[1024,128]{1,0:T(8,128)}, f32[3,4,128]{2,1,0:T(4,128)}) custom-call(f32[1024,128]{1,0:T(8,128)} %get-tuple-element.6.sol_in, f32[3,4,128]{2,1,0:T(4,128)} %get-tuple-element.7.hess_in), custom_call_target="tpu_custom_call" | custom-call | tf_op jit(solution)/shard_map/pallas_call | solution.py:831

commit v8 on v7

--- a/solution.py
+++ b/solution.py
@@ -156,6 +156,7 @@
     fresh_m,
     fresh_a,
     applied,
+    root_w,
     load_sem,
     a_ss,
     a_rs,
@@ -317,6 +318,24 @@
         total = jnp.where(lane >= RANK - COLS, total, jnp.zeros_like(total))
         return jnp.concatenate([jnp.zeros((SLICE, COLS), F32), total], axis=1)
 
+    def compose(op):
+        def step(h, own):
+            side = pl.multiple_of(own % 2 * LANES, LANES)
+            return trans[op, h, pl.ds(side, LANES), :]
+
+        path = jnp.dot(step(3, zc), step(4, zc // 2), preferred_element_type=F32)
+        path = product_rows(path, step(5, zc // 4), NN)
+        near = product_rows(path, coup[op, 6, xc % 2], NN)
+        far = product_rows(path, step(6, xc), NN)
+        far = product_rows(far, coup[op, 7, xc // 2], NN)
+        pieces = [near]
+        for s in range(2):
+            pieces.append(product_rows(far, trans[op, 6, s * LANES : (s + 1) * LANES, :], NT))
+        for i, piece in enumerate(pieces):
+            high, low = halves(piece.T)
+            root_w[op, 0, i * LANES : (i + 1) * LANES, :] = high
+            root_w[op, 1, i * LANES : (i + 1) * LANES, :] = low
+
     def leaf_terms(op, value, sums=None, only_stack=False):
         high, low = halves(value)
         stacked[:, :COLS] = high
@@ -410,17 +429,20 @@
         near3 = own_bridge(lambda n: z_slot[op, n], zc, op, 3)
         near4 = own_bridge(lambda n: c4_ref[n], zc // 2, op, 4)
         near5 = own_bridge(lambda n: c5_ref[n], zc // 4, op, 5)
+        near = near3 + own_down(near4 + own_down(near5, zc // 2, op, 4), zc, op, 3)
         if while_x is not None:
             while_x()
         arrived(x)
-        c7 = upward(x_slot[op], op, 6)
-        near6 = own_bridge(lambda n: x_slot[op, n], xc, op, 6)
-        c4_ref[0:2] = c7
-        d7 = own_bridge(lambda n: c4_ref[n], xc // 2, op, 7)
-        d6 = near6 + own_down(d7, xc, op, 6)
-        d5 = near5 + own_down(d6, zc // 4, op, 5)
-        d4 = near4 + own_down(d5, zc // 2, op, 4)
-        d3 = near3 + own_down(d4, zc, op, 3)
+        other = 2 * (1 - xc // 2)
+        above = jnp.concatenate(
+            [x_slot[op, xc + 1 - 2 * (xc % 2)], x_slot[op, other], x_slot[op, other + 1]], axis=1
+        )
+        high, low = halves(above)
+        main = jnp.dot(
+            jnp.concatenate([high, low], axis=0), root_w[op, 0], preferred_element_type=F32
+        )
+        rest = jnp.dot(high, root_w[op, 1], preferred_element_type=F32)
+        d3 = near + main[:SLICE] + main[SLICE:] + rest
         d2 = downward(bridge2[...], d3.reshape(1, SLICE, LANES), op, 2)
         d1 = downward(bridge1[...], d2, op, 1)
         d0 = downward(bridge0[...], d1, op, 0)
@@ -590,7 +612,8 @@
 
         def in_m_tree():
             at_first(
-                lambda: pad_tree(0, 3, LEVELS), lambda: pad_tree(1, 0, LEVELS), lambda: turn_rows(0)
+                lambda: pad_tree(0, 3, LEVELS), lambda: compose(0),
+                lambda: pad_tree(1, 0, LEVELS), lambda: turn_rows(0),
             )
 
             @pl.when(j > 0)
@@ -613,7 +636,7 @@
             fresh_a[i] = a_slot[1, i] + joined_rows(0, low[i], i)
 
         def in_a_tree():
-            at_first(lambda: turn_rows(1))
+            at_first(lambda: turn_rows(1), lambda: compose(1))
             d = down_copies(0)
             finished(d)
 
@@ -791,6 +814,7 @@
         pltpu.VMEM(tree[1:], F32),
         pltpu.VMEM(tree[1:], F32),
         pltpu.VMEM((ITERS - 1, WIDTH, COLS), F32),
+        pltpu.VMEM((2, 2, 3 * LANES, LANES), BF16),
         dma((11,)),
         dma((2, GROUP - 1)),
         dma((2, GROUP - 1)),

time: 106 us -> 104 us (0.981)
  Pallas kernels: 106 us -> 103 us
    pallas_call x1, Pallas kernels: 104 us -> 101 us  [on_device(): pl.pallas_call(kernel, out_shape=(jax.ShapeDtypeStruct((WIDTH, COLS), F32...]
where the time goes in v8:
time: 104 us
  Pallas kernels  103 us (99%)
    pallas_call x1, Pallas kernels, on_device(): pl.pallas_call(kernel, out_shape=(jax.ShapeDtypeStruct((WIDTH, COLS), F32...  101 us

profile of v8, /device:TPU:1, one launch (start us, length us, event | category | flops | bytes accessed | tf_op | source)
XLA Modules:
  0.0 103.8 jit_solution(4696218460866151212)
XLA Ops:
  0.6 101.3 %shard_map.122 = (f32[1024,128]{1,0:T(8,128)}, f32[3,4,128]{2,1,0:T(4,128)}) custom-call(f32[1024,128]{1,0:T(8,128)} %rhs_hbm.1, bf16[1,1024,1024]{2,1,0:T(8,128)(2,1)} %ea_hbm.1, bf16[1,200,1024]{2,1,0:T(8,128)(2,1)} %pa_hbm.1, bf16[1,200,1024]{2,1,0:T(8,128)(2,1)} %qa_hbm.1, bf16[8,2,200,200]{3,2,1,0:T(8,128)(2,1)} %ta_hbm.1, ...), custom_call_target="tpu_custom_call" | custom-call | tf_op jit(solution)/shard_map/pallas_call | solution.py:842
  102.0 1.9 %shard_map.123 = (f32[1024,128]{1,0:T(8,128)}, f32[3,4,128]{2,1,0:T(4,128)}) custom-call(f32[1024,128]{1,0:T(8,128)} %get-tuple-element.6.sol_in, f32[3,4,128]{2,1,0:T(4,128)} %get-tuple-element.7.hess_in), custom_call_target="tpu_custom_call" | custom-call | tf_op jit(solution)/shard_map/pallas_call | solution.py:855

commit v9 on v8

--- a/solution.py
+++ b/solution.py
@@ -483,23 +483,28 @@
         for c in join_copies(op)[0]:
             c.start()
 
+    def ready_joins(op, first):
+        def one(k, carry):
+            i = (first + 2 * k) % GROUP
+            high, low = halves(jnp.pad(joins[op, i], ((0, LANES - RANK), (0, 0))))
+            join_w[op, i, 0] = high
+            join_w[op, i, 1] = low
+            return carry
+
+        lax.fori_loop(0, GROUP // 2, one, 0)
+
     def pass_joins(op):
         for came, further in zip(join_copies(op)[1][1:], pass_copies(op)[0]):
             came.wait_recv()
             further.start()
+        ready_joins(op, g)
 
     def end_joins(op):
         join_copies(op)[1][0].wait_recv()
         for c in pass_copies(op)[1]:
             c.wait_recv()
 
-        def one(i, carry):
-            high, low = halves(jnp.pad(joins[op, i], ((0, LANES - RANK), (0, 0))))
-            join_w[op, i, 0] = high
-            join_w[op, i, 1] = low
-            return carry
-
-        lax.fori_loop(0, GROUP, one, 0)
+        ready_joins(op, partner)
         for c in join_copies(op)[0] + pass_copies(op)[0]:
             c.wait_send()
 

time: 104 us -> 104 us (level)
  no operation moved by 1% of the time
where the time goes in v9:
time: 104 us; the launch traced here: 103 us
  Pallas kernels  103 us (99%)
    pallas_call x1, Pallas kernels, on_device(): pl.pallas_call(kernel, out_shape=(jax.ShapeDtypeStruct((WIDTH, COLS), F32...  101 us

profile of v9, /device:TPU:1, one launch (start us, length us, event | category | flops | bytes accessed | tf_op | source)
XLA Modules:
  0.0 103.4 jit_solution(15022330646638854226)
XLA Ops:
  0.6 100.9 %shard_map.122 = (f32[1024,128]{1,0:T(8,128)}, f32[3,4,128]{2,1,0:T(4,128)}) custom-call(f32[1024,128]{1,0:T(8,128)} %rhs_hbm.1, bf16[1,1024,1024]{2,1,0:T(8,128)(2,1)} %ea_hbm.1, bf16[1,200,1024]{2,1,0:T(8,128)(2,1)} %pa_hbm.1, bf16[1,200,1024]{2,1,0:T(8,128)(2,1)} %qa_hbm.1, bf16[8,2,200,200]{3,2,1,0:T(8,128)(2,1)} %ta_hbm.1, ...), custom_call_target="tpu_custom_call" | custom-call | tf_op jit(solution)/shard_map/pallas_call | solution.py:847
  101.6 1.9 %shard_map.123 = (f32[1024,128]{1,0:T(8,128)}, f32[3,4,128]{2,1,0:T(4,128)}) custom-call(f32[1024,128]{1,0:T(8,128)} %get-tuple-element.6.sol_in, f32[3,4,128]{2,1,0:T(4,128)} %get-tuple-element.7.hess_in), custom_call_target="tpu_custom_call" | custom-call | tf_op jit(solution)/shard_map/pallas_call | solution.py:860
